TPU v7x, 256 devices: a 4x2x16 block of a 4x16x16 slice. The times are simulated.
256 devices in a mesh: rep: 2 (over y), seq: 16 (over z), section: 2 (over core), head: 4 (over x).
Axes of the slice: x: 4, y: 2, z: 16, core: 2. Of those that a mesh axis runs over, the one named last changes fastest.
The devices are a block of a 4x16x16 slice.
Arguments:
- hidden: bfloat16 [6, 1024, 2048], P('rep', 'seq'), parts along dimension 0, may hold values from -6 to 6
- lengths: int32 [6], P('rep'), parts along dimension 0, may hold values from 1 to 1024, 2304 in all
- attn_gain: float32 [2, 2048], P('section'), may hold values from 0.1 to 1.9
- w_query: bfloat16 [2, 2048, 2048], P('section', None, 'head'), may hold values from -2 to 2
- w_latent: bfloat16 [2, 2048, 512], P('section'), may hold values from -0.125 to 0.125
- latent_gain: float32 [2, 512], P('section'), may hold values from 0.1 to 1.9
- w_key: bfloat16 [2, 512, 2048], P('section', None, 'head'), may hold values from -0.25 to 0.25
- w_value: bfloat16 [2, 512, 2048], P('section', None, 'head'), may hold values from -0.25 to 0.25
- w_out: bfloat16 [2, 2048, 2048], P('section', 'head'), may hold values from -0.125 to 0.125
Outputs:
- final: float32 [6, 1024, 2048], P('rep', ('seq', 'head'), 'section'), parts along dimension 0
- latents: float32 [2, 6, 1024, 512], P('section', 'rep', 'seq'), parts along dimension 1
There are 2 independent parts, one for each index of `rep`. A program takes and returns all parts, laid end to end along the dimension named above; an argument that names none is the same for every part. Nothing has to cross between parts.
Inputs may be any that keep to these rules, and one draw needn't show every extreme that they name: lengths sum to 2304 and one block holds exactly 1024; the live tokens of a block are its first slots.
All inputs are finite; a program needn't handle non-finite values.
Results may differ from a plain program's by a relative error of at most 0.015.
The roundings to bfloat16 on the way count: a program that leaves them out, or rounds other values in their place, can miss the bound.
Values may be sent and summed in bfloat16 or wider, within the bound.
A program may use at most 128 MiB of HBM per device.

v0:
```python
import jax
import jax.numpy as jnp
from jax import lax
from jax.sharding import PartitionSpec as P

HD = 128


def from_everyone(value, axis):
    copies = jnp.broadcast_to(value, (lax.axis_size(axis), *value.shape))
    return lax.all_to_all(copies, axis, split_axis=0, concat_axis=0, tiled=True)


def in_order(tiles, dim):
    dims = list(tiles.shape[1:])
    dims[dim] *= tiles.shape[0]
    return jnp.moveaxis(tiles, 0, dim).reshape(dims)


def gather_directly(value, axis, dim):
    tiles = from_everyone(value, axis)
    return in_order(tiles, dim)


def over_copies(value, axis):
    return from_everyone(value, axis).astype(jnp.float32).sum(axis=0)


def shifted(value, axis, by):
    length = lax.axis_size(axis)
    pairs = [(i, i + by) for i in range(length) if 0 <= i + by < length]
    return lax.ppermute(value, axis, pairs)


def broadcast(value, axis, root):
    return lax.dynamic_index_in_dim(lax.all_gather(value, axis), root, 0, keepdims=False)


def rms_scale(values, gain):
    mean_sq = jnp.mean(values * values, axis=-1, keepdims=True)
    return values * lax.rsqrt(mean_sq + 1e-06) * gain


def visible(group, lengths, query_pos, key_pos, blocks):
    block_ids = jnp.arange(blocks, dtype=jnp.int32)
    past = (block_ids < group)[:, None] & (key_pos[None, :] < lengths[:blocks, None])
    same = (block_ids == group)[None, :, None] & (
        key_pos[None, None, :] <= query_pos[:, None, None]
    )
    return past[None] | same


def online_step(carry, scores, mask, latent_piece):
    top, total, accum = carry
    scores = jnp.where(mask[None], scores, -1e30)
    new_top = jnp.maximum(top, jnp.max(scores, axis=(2, 3)))
    weights = jnp.where(mask[None], jnp.exp(scores - new_top[:, :, None, None]), 0.0)
    total = jnp.sum(weights, axis=(2, 3))
    rounded = weights.astype(jnp.bfloat16)
    gained = jnp.einsum("hqck,ckr->hqr", rounded, latent_piece, preferred_element_type=jnp.float32)
    accum = gained
    return (new_top, total, accum)


def shards(hidden, lengths, attn_gain, w_query, w_latent, latent_gain, w_key, w_value, w_out):
    sections = lax.axis_size("section")
    section_id = lax.axis_index("section")
    seq_id = lax.axis_index("seq")
    seq_count = lax.axis_size("seq")
    head_count = lax.axis_size("head")
    head_id = lax.axis_index("head")
    groups, rows, width = hidden.shape
    layers_here = w_query.shape[0]
    rank = w_latent.shape[2]
    heads_here = w_key.shape[2] // HD
    query_cols = heads_here * HD
    share = rows // head_count
    scale = 1.0 / HD**0.5
    query_pos = seq_id * rows + jnp.arange(rows, dtype=jnp.int32)
    full_cache = jnp.zeros((layers_here, groups, rows * seq_count, rank), jnp.bfloat16)
    own_store = jnp.zeros((layers_here, groups, rows, rank), jnp.float32)
    finals = jnp.zeros((groups, rows, width), jnp.float32)
    incoming = jnp.zeros((rows, width), jnp.float32)
    ticks = groups + sections - 1
    for tick in range(ticks):
        blocks = min(tick, groups - 1) + 1
        group = tick - section_id
        active = (group >= 0) & (group < groups)
        group_at = jnp.clip(group, 0, groups - 1)
        own = lax.dynamic_index_in_dim(hidden, group_at, 0, keepdims=False)
        state = jnp.where(section_id == 0, own.astype(jnp.float32), incoming)
        normed_part = rms_scale(state, attn_gain[0]).astype(jnp.bfloat16)
        query_weight = w_query[0]
        latent_weight = w_latent[0]
        query_full = jnp.dot(normed_part, query_weight, preferred_element_type=jnp.float32)
        raw = jnp.dot(normed_part, latent_weight, preferred_element_type=jnp.float32)
        query = query_full.astype(jnp.bfloat16).reshape(rows, heads_here, HD)
        latent_full = rms_scale(raw, latent_gain[0])
        latent = latent_full.astype(jnp.bfloat16)
        kept = own_store[0, group_at]
        own_store = own_store.at[0, group_at].set(jnp.where(active, latent_full, kept))
        key_map = w_key[0].reshape(rank, heads_here, HD)
        value_map = w_value[0].reshape(rank, heads_here, HD)
        absorbed = jnp.einsum("qhd,rhd->hqr", query, key_map, preferred_element_type=jnp.float32)
        absorbed = (absorbed * scale).astype(jnp.bfloat16)
        init = (
            jnp.full((heads_here, rows), -1e30, jnp.float32),
            jnp.zeros((heads_here, rows), jnp.float32),
            jnp.zeros((heads_here, rows, rank), jnp.float32),
        )
        gathered = gather_directly(latent, "seq", 0)
        current = full_cache[0, group_at]
        full_cache = full_cache.at[0, group_at].set(jnp.where(active, gathered, current))
        piece = full_cache[0, :blocks]
        key_pos = jnp.arange(piece.shape[1], dtype=jnp.int32)
        mask = visible(group, lengths, query_pos, key_pos, piece.shape[0])
        scores = jnp.einsum("hqr,ckr->hqck", absorbed, piece, preferred_element_type=jnp.float32)
        top, total, accum = online_step(init, scores, mask, piece)
        context = (accum / total[:, :, None]).astype(jnp.bfloat16)
        attn = jnp.einsum("hqr,rhd->qhd", context, value_map, preferred_element_type=jnp.float32)
        attn = attn.astype(jnp.bfloat16).reshape(rows, query_cols)
        out_weight = w_out[0]
        partial_out = jnp.dot(attn, out_weight, preferred_element_type=jnp.float32)
        summed = over_copies(partial_out.astype(jnp.bfloat16), "head").astype(jnp.float32)
        state = state + summed
        keep_final = active & (section_id == sections - 1)
        finals = finals.at[group_at].set(jnp.where(keep_final, state, finals[group_at]))
        if tick + 1 < ticks:
            incoming = shifted(state.astype(jnp.bfloat16), "section", 1).astype(state.dtype)
    mine = lax.dynamic_slice_in_dim(finals, head_id * share, share, 1)
    mine = broadcast(mine.astype(jnp.bfloat16), "section", sections - 1).astype(mine.dtype)
    out_pos = seq_id * rows + head_id * share + jnp.arange(share, dtype=jnp.int32)
    live_rows = out_pos[None, :] < lengths[:, None]
    mine = jnp.where(live_rows[:, :, None], mine, jnp.zeros_like(mine))
    part_width = width // sections
    final = lax.dynamic_slice_in_dim(mine, section_id * part_width, part_width, 2)
    live = query_pos[None, :] < lengths[:, None]
    stored = jnp.where(live[None, :, :, None], own_store, jnp.zeros_like(own_store))
    return (final, stored)


def solution(mesh):
    return jax.shard_map(
        shards,
        mesh=mesh,
        in_specs=(
            P("rep", "seq", None),
            P("rep"),
            P("section", None),
            P("section", None, "head"),
            P("section", None, None),
            P("section", None),
            P("section", None, "head"),
            P("section", None, "head"),
            P("section", "head", None),
        ),
        out_specs=(P("rep", ("seq", "head"), "section"), P("section", "rep", "seq", None)),
        check_vma=False,
    )
```

profile of v0, /device:TPU:33, one launch (start us, length us, event | category | flops | bytes accessed | tf_op | source)
XLA Modules:
  0.0 415.6 jit_solution(4242450852916493947)
XLA Ops:
  6.4 24.5 %all-to-all-start = ((bf16[16,64,512]{2,1,0:T(8,128)(2,1)}), bf16[16,64,512]{2,1,0:T(8,128)(2,1)}, u32[]{:S(2)}, u32[]{:S(2)}) async-start(bf16[16,64,512]{2,1,0:T(8,128)(2,1)} %broadcast_in_dim.100), calls=%async_computation | async-start | bytes 2097152 | tf_op jit(solution)/shard_map/all_to_all | solution.py:11
  37.9 37.8 %all-to-all-done = bf16[16,64,512]{2,1,0:T(8,128)(2,1)} async-done(((bf16[16,64,512]{2,1,0:T(8,128)(2,1)}), bf16[16,64,512]{2,1,0:T(8,128)(2,1)}, u32[]{:S(2)}, u32[]{:S(2)}) %all-to-all-start) | async-done | bytes 1048608 | tf_op jit(solution)/shard_map/all_to_all | solution.py:11
  79.4 3.0 fusion.241
  87.0 14.0 %all_to_all.40 = bf16[4,64,2048]{2,1,0:T(8,128)(2,1)S(1)} all-to-all(bf16[4,64,2048]{2,1,0:T(8,128)(2,1)S(1)} %broadcast_in_dim.103), channel_id=1, replica_groups=mesh['rep'=2,'seq'=16,'section'=2,'head'=4] {'head'}, dimensions={0} | all-to-all | bytes 2097152 | tf_op jit(solution)/shard_map/all_to_all | solution.py:11
  102.5 9.5 %collective-permute-done = bf16[64,2048]{1,0:T(8,128)(2,1)S(1)} collective-permute-done((bf16[64,2048]{1,0:T(8,128)(2,1)S(1)}, bf16[64,2048]{1,0:T(8,128)(2,1)S(1)}, u32[]{:S(2)}, u32[]{:S(2)}) %collective-permute-start) | collective-permute-done | bytes 262176 | tf_op jit(solution)/shard_map/ppermute | solution.py:32
  114.1 11.1 %all-to-all-start.2 = ((bf16[16,64,512]{2,1,0:T(8,128)(2,1)}), bf16[16,64,512]{2,1,0:T(8,128)(2,1)}, u32[]{:S(2)}, u32[]{:S(2)}) async-start(bf16[16,64,512]{2,1,0:T(8,128)(2,1)} %broadcast_in_dim.108), calls=%async_computation.2 | async-start | bytes 2097152 | tf_op jit(solution)/shard_map/all_to_all | solution.py:11
  127.6 44.0 %all-to-all-done.2 = bf16[16,64,512]{2,1,0:T(8,128)(2,1)} async-done(((bf16[16,64,512]{2,1,0:T(8,128)(2,1)}), bf16[16,64,512]{2,1,0:T(8,128)(2,1)}, u32[]{:S(2)}, u32[]{:S(2)}) %all-to-all-start.2) | async-done | bytes 1048608 | tf_op jit(solution)/shard_map/all_to_all | solution.py:11
  171.6 3.4 fusion.95
  175.0 4.1 select_reduce_fusion.2
  181.3 3.2 fusion.79
  185.1 13.2 %all_to_all.41 = bf16[4,64,2048]{2,1,0:T(8,128)(2,1)S(1)} all-to-all(bf16[4,64,2048]{2,1,0:T(8,128)(2,1)S(1)} %broadcast_in_dim.111), channel_id=1, replica_groups=mesh['rep'=2,'seq'=16,'section'=2,'head'=4] {'head'}, dimensions={0} | all-to-all | bytes 2097152 | tf_op jit(solution)/shard_map/all_to_all | solution.py:11
  201.4 6.5 %collective-permute-done.1 = bf16[64,2048]{1,0:T(8,128)(2,1)S(1)} collective-permute-done((bf16[64,2048]{1,0:T(8,128)(2,1)}, bf16[64,2048]{1,0:T(8,128)(2,1)S(1)}, u32[]{:S(2)}, u32[]{:S(2)}) %collective-permute-start.1) | collective-permute-done | bytes 262176 | tf_op jit(solution)/shard_map/ppermute | solution.py:32
  212.2 11.8 %all-to-all-start.4 = ((bf16[16,64,512]{2,1,0:T(8,128)(2,1)}), bf16[16,64,512]{2,1,0:T(8,128)(2,1)}, u32[]{:S(2)}, u32[]{:S(2)}) async-start(bf16[16,64,512]{2,1,0:T(8,128)(2,1)} %broadcast_in_dim.113), calls=%async_computation.4 | async-start | bytes 2097152 | tf_op jit(solution)/shard_map/all_to_all | solution.py:11
  227.4 2.7 fusion.85
  230.2 40.2 %all-to-all-done.4 = bf16[16,64,512]{2,1,0:T(8,128)(2,1)} async-done(((bf16[16,64,512]{2,1,0:T(8,128)(2,1)}), bf16[16,64,512]{2,1,0:T(8,128)(2,1)}, u32[]{:S(2)}, u32[]{:S(2)}) %all-to-all-start.4) | async-done | bytes 1048608 | tf_op jit(solution)/shard_map/all_to_all | solution.py:11
  270.4 3.4 fusion.96
  273.8 5.5 %select_reduce_fusion.1 = (f32[4,64]{1,0:T(4,128)}, f32[4,64,3,1024]{3,1,2,0:T(8,128)}) fusion(pred[64,3,1024]{2,0,1:T(8,128)(4,1)} %get-tuple-element.155, bf16[1,3,1024,512]{3,2,1,0:T(8,128)(2,1)} %fusion.96, bf16[512,4,128]{2,1,0:T(4,128)(2,1)} %reshape_squeeze.4, bf16[8,4,8,128]{3,2,1,0:T(8,128)(2,1)} %fusion.85), kind=kOutput, calls=%fused_computation.11 | convolution fusion | flops 840695552 | bytes 7078912 | tf_op jit(solution)/shard_map/hqr,ckr->hqck/dot_general | solution.py:117
  280.1 3.4 fusion.8
  283.4 4.8 %fusion.80 = bf16[4,8,8,128]{3,2,1,0:T(8,128)(2,1)} fusion(bf16[1,3,1024,512]{3,2,1,0:T(8,128)(2,1)} %fusion.96, f32[4,64,3,1024]{3,1,2,0:T(8,128)} %get-tuple-element.173, f32[4,64]{1,0:T(4,128)S(1)} %broadcast_maximum_fusion.1, pred[64,3,1024]{2,0,1:T(8,128)(4,1)} %get-tuple-element.155, bf16[512,4,128]{2,1,0:T(4,128)(2,1)} %reshape_squeeze.5, ...), kind=kOutput, calls=%fused_computation.89 | convolution fusion | flops 842301440 | bytes 7079936 | tf_op jit(solution)/shard_map/hqr,rhd->qhd/dot_general | solution.py:120
  289.7 13.3 %all_to_all.42 = bf16[4,64,2048]{2,1,0:T(8,128)(2,1)S(1)} all-to-all(bf16[4,64,2048]{2,1,0:T(8,128)(2,1)S(1)} %broadcast_in_dim.200), channel_id=1, replica_groups=mesh['rep'=2,'seq'=16,'section'=2,'head'=4] {'head'}, dimensions={0} | all-to-all | bytes 2097152 | tf_op jit(solution)/shard_map/all_to_all | solution.py:11
  304.6 6.3 %collective-permute-done.2 = bf16[64,2048]{1,0:T(8,128)(2,1)S(1)} collective-permute-done((bf16[64,2048]{1,0:T(8,128)(2,1)S(1)}, bf16[64,2048]{1,0:T(8,128)(2,1)S(1)}, u32[]{:S(2)}, u32[]{:S(2)}) %collective-permute-start.2) | collective-permute-done | bytes 262176 | tf_op jit(solution)/shard_map/ppermute | solution.py:32
  313.6 11.8 %all-to-all-start.6 = ((bf16[16,64,512]{2,1,0:T(8,128)(2,1)}), bf16[16,64,512]{2,1,0:T(8,128)(2,1)}, u32[]{:S(2)}, u32[]{:S(2)}) async-start(bf16[16,64,512]{2,1,0:T(8,128)(2,1)} %broadcast_in_dim.202), calls=%async_computation.6 | async-start | bytes 2097152 | tf_op jit(solution)/shard_map/all_to_all | solution.py:11
  336.8 3.9 copy.147
  341.3 30.5 %all-to-all-done.6 = bf16[16,64,512]{2,1,0:T(8,128)(2,1)} async-done(((bf16[16,64,512]{2,1,0:T(8,128)(2,1)}), bf16[16,64,512]{2,1,0:T(8,128)(2,1)}, u32[]{:S(2)}, u32[]{:S(2)}) %all-to-all-start.6) | async-done | bytes 1048608 | tf_op jit(solution)/shard_map/all_to_all | solution.py:11
  371.8 3.5 fusion.98
  375.3 4.9 %select_reduce_fusion = (f32[4,64]{1,0:T(4,128)S(1)}, f32[4,64,3,1024]{3,1,2,0:T(8,128)}) fusion(pred[64,3,1024]{2,0,1:T(8,128)(4,1)} %get-tuple-element.154, bf16[3,1024,512]{2,1,0:T(8,128)(2,1)} %fusion.98, bf16[512,4,128]{2,1,0:T(4,128)(2,1)} %reshape_squeeze.4, bf16[8,4,8,128]{3,2,1,0:T(8,128)(2,1)S(1)} %fusion.82), kind=kOutput, calls=%fused_computation.10 | convolution fusion | flops 840695552 | bytes 7078912 | tf_op jit(solution)/shard_map/hqr,ckr->hqck/dot_general | solution.py:117
  380.2 2.8 fusion.10
  383.0 4.2 %fusion.81 = bf16[4,8,8,128]{3,2,1,0:T(8,128)(2,1)S(1)} fusion(bf16[3,1024,512]{2,1,0:T(8,128)(2,1)} %fusion.98, f32[4,64,3,1024]{3,1,2,0:T(8,128)} %get-tuple-element.177, f32[4,64]{1,0:T(4,128)S(1)} %broadcast_maximum_fusion, pred[64,3,1024]{2,0,1:T(8,128)(4,1)} %get-tuple-element.154, bf16[512,4,128]{2,1,0:T(4,128)(2,1)} %reshape_squeeze.5, ...), kind=kOutput, calls=%fused_computation.90 | convolution fusion | flops 842301440 | bytes 7079936 | tf_op jit(solution)/shard_map/hqr,rhd->qhd/dot_general | solution.py:120
  388.9 4.3 %all-to-all-start.7 = ((bf16[4,64,2048]{2,1,0:T(8,128)(2,1)}), bf16[4,64,2048]{2,1,0:T(8,128)(2,1)}, u32[]{:S(2)}, u32[]{:S(2)}) async-start(bf16[4,64,2048]{2,1,0:T(8,128)(2,1)} %broadcast_in_dim.203), calls=%async_computation.7 | async-start | bytes 2097152 | tf_op jit(solution)/shard_map/all_to_all | solution.py:11
  393.2 2.6 fusion.145
  401.0 3.0 all-to-all-done.7
  407.8 7.1 %all-gather = bf16[6,16,2048]{2,1,0:T(8,128)(2,1)S(1)} all-gather(bf16[3,16,2048]{2,1,0:T(8,128)(2,1)S(1)} %dynamic-slice_convert_fusion), channel_id=2, replica_groups=mesh['rep'=2,'seq'=16,'section'=2,'head'=4] {'section'}, dimensions={0}, use_global_device_ids=true | all-gather | bytes 589824 | tf_op jit(solution)/shard_map/all_gather | solution.py:36
  (165 shorter events, 69.6 us)
Async XLA Ops:
  0.6 85.7 %copy-start = (bf16[1,512,2048]{2,1,0:T(8,128)(2,1)S(1)}, bf16[1,512,2048]{2,1,0:T(8,128)(2,1)}, u32[]{:S(2)}) copy-start(bf16[1,512,2048]{2,1,0:T(8,128)(2,1)} %param.41) | copy-start | bytes 6291460
  4.3 33.5 %copy-start.17 = (f32[64,512]{1,0:T(8,128)}, f32[64,512]{1,0:T(8,128)S(1)}, u32[]{:S(2)}) copy-start(f32[64,512]{1,0:T(8,128)S(1)} %get-tuple-element.163) | copy-start | bytes 393220
  4.3 30.6 %copy-start.21 = (s32[3]{0:T(128)S(1)}, s32[3]{0:T(128)}, u32[]{:S(2)}) copy-start(s32[3]{0:T(128)} %param.34) | copy-start | bytes 40
  4.3 30.6 %copy-start.29 = (s32[4]{0:T(128)S(1)}, s32[4]{0:T(128)}, u32[]{:S(2)}) copy-start(s32[4]{0:T(128)} %constant.327.clone.1) | copy-start | bytes 52
  4.3 31.3 %copy-start.4 = (bf16[3,64,2048]{2,1,0:T(8,128)(2,1)S(1)}, bf16[3,64,2048]{2,1,0:T(8,128)(2,1)}, u32[]{:S(2)}) copy-start(bf16[3,64,2048]{2,1,0:T(8,128)(2,1)} %param.33) | copy-start | bytes 2359300
  4.3 31.3 %copy-start.19 = (f32[1,2048]{1,0:T(1,128)S(1)}, f32[1,2048]{1,0:T(1,128)}, u32[]{:S(2)}) copy-start(f32[1,2048]{1,0:T(1,128)} %param.35) | copy-start | bytes 24580
  4.4 30.5 %copy-start.23 = (f32[64]{0:T(128)}, f32[64]{0:T(128)S(1)}, u32[]{:S(2)}) copy-start(f32[64]{0:T(128)S(1)} %add_rsqrt_fusion.6) | copy-start | bytes 772
  6.4 69.4 %all-to-all-start = ((bf16[16,64,512]{2,1,0:T(8,128)(2,1)}), bf16[16,64,512]{2,1,0:T(8,128)(2,1)}, u32[]{:S(2)}, u32[]{:S(2)}) async-start(bf16[16,64,512]{2,1,0:T(8,128)(2,1)} %broadcast_in_dim.100), calls=%async_computation | async-start | bytes 2097152 | tf_op jit(solution)/shard_map/all_to_all | solution.py:11
  34.8 43.5 %copy-start.33 = (s32[64]{0:T(128)}, s32[64]{0:T(128)S(1)}, u32[]{:S(2)}) copy-start(s32[64]{0:T(128)S(1)} %iota_add_fusion) | copy-start | bytes 772
  37.9 87.4 %copy-start.18 = (pred[64,1024]{1,0:T(8,128)(4,1)}, pred[64,1024]{1,0:T(8,128)(4,1)S(1)}, u32[]{:S(2)}) copy-start(pred[64,1024]{1,0:T(8,128)(4,1)S(1)} %get-tuple-element.160) | copy-start | bytes 196612
  86.8 25.4 %copy-start.1 = (bf16[1,2048,512]{2,1,0:T(8,128)(2,1)S(1)}, bf16[1,2048,512]{2,1,0:T(8,128)(2,1)}, u32[]{:S(2)}) copy-start(bf16[1,2048,512]{2,1,0:T(8,128)(2,1)} %param.37) | copy-start | bytes 6291460
  101.0 11.9 %copy-start.20 = (f32[1,512]{1,0:T(1,128)S(1)}, f32[1,512]{1,0:T(1,128)}, u32[]{:S(2)}) copy-start(f32[1,512]{1,0:T(1,128)} %param.38) | copy-start | bytes 6148
  101.1 11.7 %copy-start.5 = (f32[64,2048]{1,0:T(8,128)}, f32[64,2048]{1,0:T(8,128)S(1)}, u32[]{:S(2)}) copy-start(f32[64,2048]{1,0:T(8,128)S(1)} %convert_reduce_fusion.3) | copy-start | bytes 1572868
  101.2 10.8 %collective-permute-start = (bf16[64,2048]{1,0:T(8,128)(2,1)S(1)}, bf16[64,2048]{1,0:T(8,128)(2,1)S(1)}, u32[]{:S(2)}, u32[]{:S(2)}) collective-permute-start(bf16[64,2048]{1,0:T(8,128)(2,1)S(1)} %fusion.151), channel_id=1, source_target_pairs={{0,4},{1,5},{2,6},{3,7},{8,12},{9,13},{10,14},{11,15},{16,20},{17,... | collective-permute-start | bytes 786440 | tf_op jit(solution)/shard_map/ppermute | solution.py:32
  112.9 12.5 %copy-start.24 = (f32[64]{0:T(128)}, f32[64]{0:T(128)S(1)}, u32[]{:S(2)}) copy-start(f32[64]{0:T(128)S(1)} %add_rsqrt_fusion.4) | copy-start | bytes 772
  114.1 57.5 %all-to-all-start.2 = ((bf16[16,64,512]{2,1,0:T(8,128)(2,1)}), bf16[16,64,512]{2,1,0:T(8,128)(2,1)}, u32[]{:S(2)}, u32[]{:S(2)}) async-start(bf16[16,64,512]{2,1,0:T(8,128)(2,1)} %broadcast_in_dim.108), calls=%async_computation.2 | async-start | bytes 2097152 | tf_op jit(solution)/shard_map/all_to_all | solution.py:11
  200.1 7.9 %collective-permute-start.1 = (bf16[64,2048]{1,0:T(8,128)(2,1)}, bf16[64,2048]{1,0:T(8,128)(2,1)S(1)}, u32[]{:S(2)}, u32[]{:S(2)}) collective-permute-start(bf16[64,2048]{1,0:T(8,128)(2,1)} %fusion.182), channel_id=1, source_target_pairs={{0,4},{1,5},{2,6},{3,7},{8,12},{9,13},{10,14},{11,15},{16,20},{17,... | collective-permute-start | bytes 786440 | tf_op jit(solution)/shard_map/ppermute | solution.py:32
  212.2 58.2 %all-to-all-start.4 = ((bf16[16,64,512]{2,1,0:T(8,128)(2,1)}), bf16[16,64,512]{2,1,0:T(8,128)(2,1)}, u32[]{:S(2)}, u32[]{:S(2)}) async-start(bf16[16,64,512]{2,1,0:T(8,128)(2,1)} %broadcast_in_dim.113), calls=%async_computation.4 | async-start | bytes 2097152 | tf_op jit(solution)/shard_map/all_to_all | solution.py:11
  289.6 21.6 %copy-start.2 = (bf16[1,2048,512]{2,1,0:T(8,128)(2,1)S(1)}, bf16[1,2048,512]{2,1,0:T(8,128)(2,1)}, u32[]{:S(2)}) copy-start(bf16[1,2048,512]{2,1,0:T(8,128)(2,1)} %param.37) | copy-start | bytes 6291460
  303.2 8.6 %copy-start.8 = (f32[64,2048]{1,0:T(8,128)}, f32[64,2048]{1,0:T(8,128)S(1)}, u32[]{:S(2)}) copy-start(f32[64,2048]{1,0:T(8,128)S(1)} %convert_reduce_fusion.1) | copy-start | bytes 1572868
  303.3 7.7 %collective-permute-start.2 = (bf16[64,2048]{1,0:T(8,128)(2,1)S(1)}, bf16[64,2048]{1,0:T(8,128)(2,1)S(1)}, u32[]{:S(2)}, u32[]{:S(2)}) collective-permute-start(bf16[64,2048]{1,0:T(8,128)(2,1)S(1)} %fusion.181), channel_id=1, source_target_pairs={{0,4},{1,5},{2,6},{3,7},{8,12},{9,13},{10,14},{11,15},{16,20},{17,... | collective-permute-start | bytes 786440 | tf_op jit(solution)/shard_map/ppermute | solution.py:32
  311.1 17.5 %copy-start.22 = (s32[3]{0:T(128)S(1)}, s32[3]{0:T(128)}, u32[]{:S(2)}) copy-start(s32[3]{0:T(128)} %param.34) | copy-start | bytes 40
  313.6 58.2 %all-to-all-start.6 = ((bf16[16,64,512]{2,1,0:T(8,128)(2,1)}), bf16[16,64,512]{2,1,0:T(8,128)(2,1)}, u32[]{:S(2)}, u32[]{:S(2)}) async-start(bf16[16,64,512]{2,1,0:T(8,128)(2,1)} %broadcast_in_dim.202), calls=%async_computation.6 | async-start | bytes 2097152 | tf_op jit(solution)/shard_map/all_to_all | solution.py:11
  325.4 8.3 %copy-start.7 = (f32[64,2048]{1,0:T(8,128)S(1)}, f32[64,2048]{1,0:T(8,128)}, u32[]{:S(2)}) copy-start(f32[64,2048]{1,0:T(8,128)} %copy-done.6) | copy-start | bytes 1572868
  327.0 8.3 %copy-start.14 = (f32[64,512]{1,0:T(8,128)S(1)}, f32[64,512]{1,0:T(8,128)}, u32[]{:S(2)}) copy-start(f32[64,512]{1,0:T(8,128)} %copy-done.13) | copy-start | bytes 393220
  327.0 8.3 %copy-start.26 = (f32[64]{0:T(128)S(1)}, f32[64]{0:T(128)}, u32[]{:S(2)}) copy-start(f32[64]{0:T(128)} %copy-done.25) | copy-start | bytes 772
  336.8 3.9 copy-start.31
  387.7 9.1 %copy-start.16 = (f32[64,512]{1,0:T(8,128)S(1)}, f32[64,512]{1,0:T(8,128)}, u32[]{:S(2)}) copy-start(f32[64,512]{1,0:T(8,128)} %copy-done.15) | copy-start | bytes 393220
  387.7 9.1 %copy-start.28 = (f32[64]{0:T(128)S(1)}, f32[64]{0:T(128)}, u32[]{:S(2)}) copy-start(f32[64]{0:T(128)} %copy-done.27) | copy-start | bytes 772
  387.7 11.4 %copy-start.35 = (pred[3,64]{1,0:T(4,128)(4,1)S(1)}, pred[3,64]{1,0:T(4,128)(4,1)}, u32[]{:S(2)}) copy-start(pred[3,64]{1,0:T(4,128)(4,1)} %broadcast_compare_fusion) | copy-start | bytes 580
  388.9 15.1 %all-to-all-start.7 = ((bf16[4,64,2048]{2,1,0:T(8,128)(2,1)}), bf16[4,64,2048]{2,1,0:T(8,128)(2,1)}, u32[]{:S(2)}, u32[]{:S(2)}) async-start(bf16[4,64,2048]{2,1,0:T(8,128)(2,1)} %broadcast_in_dim.203), calls=%async_computation.7 | async-start | bytes 2097152 | tf_op jit(solution)/shard_map/all_to_all | solution.py:11
  395.8 19.0 %copy-start.34 = (pred[3,16]{1,0:T(4,128)(4,1)S(1)}, pred[3,16]{1,0:T(4,128)(4,1)}, u32[]{:S(2)}) copy-start(pred[3,16]{1,0:T(4,128)(4,1)} %broadcast_compare_fusion.1) | copy-start | bytes 148
  (12 other events, 18.8 us)
where the time goes:
time: 417 us; the launch traced here: 416 us
  waiting for transfers between devices  178 us (43%)
  starting transfers between devices  67.4 us (16%)
  other arithmetic  50.4 us (12%)
  matrix products  48.2 us (12%)
  blocking collectives  47.5 us (11%)
  local copies, waits for them, and re-layouts  22.7 us (5%)
    all_to_all x5, waiting for transfers between devices, from_everyone(): return lax.all_to_all(copies, axis, split_axis=0, concat_axis=0, tiled=True)  156 us
    all_to_all x5, starting transfers between devices, from_everyone(): return lax.all_to_all(copies, axis, split_axis=0, concat_axis=0, tiled=True)  63.5 us
    all_to_all x3, blocking collectives, from_everyone(): return lax.all_to_all(copies, axis, split_axis=0, concat_axis=0, tiled=True)  40.4 us
    ppermute x3, waiting for transfers between devices, shifted(): return lax.ppermute(value, axis, pairs)  22.4 us
    dot_general x4, matrix products, shards(): jnp.einsum('hqr,ckr->hqck', absorbed, piece, preferred_element_type=jnp.f...  17.6 us
    dot_general x4, matrix products, shards(): jnp.einsum('hqr,rhd->qhd', context, value_map, preferred_element_type=jnp...  14.5 us
    scatter x3, other arithmetic, shards(): full_cache.at[0, group_at].set(jnp.where(active, gathered, current))  10.3 us
    reduce_sum x4, other arithmetic, online_step(): total = jnp.sum(weights, axis=(2, 3))  9.92 us
  transfers between devices with their start and end apart: 8, of which 8 were waited for; matrix products, arithmetic and copies ran while one was open for 9% of the time, Pallas kernels for 0%

commit v1 on v0

v1 whole, which is shorter than its diff:
```python
import functools

import jax
import jax.numpy as jnp
from jax import lax
from jax.experimental import pallas as pl
from jax.experimental.pallas import tpu as pltpu
from jax.sharding import PartitionSpec as P

HD = 128
EPS = 1e-06
NEG = -1e30
FAR = 1 << 30
MESH = pl.DeviceIdType.MESH
LAST = (((1,), (1,)), ((), ()))


def rms_scale(values, gain):
    mean_sq = jnp.mean(values * values, axis=-1, keepdims=True)
    return values * lax.rsqrt(mean_sq + EPS) * gain


def dot(a, b):
    return jnp.dot(a, b, preferred_element_type=jnp.float32)


def dot_t(a, b):
    return lax.dot_general(a, b, LAST, preferred_element_type=jnp.float32)


def kernel(
    nz, nx, lengths, hid_hbm, gain, wq_hbm, wl_hbm, lgain, wk_hbm, wv_hbm, wo_hbm,
    final, lat, hid, wq, wl, wk, wv, wo, normed, kv, absorbed, top, total, accum, attn,
    part, headsum, xkeep, xhalf, finsum, load_sem, r_send, r_recv, l_send, l_recv,
    rs_send, rs_recv, ag_send, ag_recv, half_send, half_recv, fin_send, fin_recv,
):
    z, x, sec = lax.axis_index("seq"), lax.axis_index("head"), lax.axis_index("section")
    other = 1 - sec
    right, left = lax.rem(z + 1, nz), lax.rem(z + nz - 1, nz)
    groups, rows, width = hid.shape
    rank = wl.shape[1]
    heads = wk.shape[1] // HD
    share = rows // nx
    mine = groups * share
    half = width // 2
    mid = nz // 2
    hrows = heads * rows

    loads = [
        pltpu.make_async_copy(src, dst, load_sem.at[i])
        for i, (src, dst) in enumerate(
            [(hid_hbm, hid), (wl_hbm.at[0], wl), (wq_hbm.at[0], wq), (wk_hbm.at[0], wk), (wv_hbm.at[0], wv), (wo_hbm.at[0], wo)]
        )
    ]
    for load in loads:
        load.start()

    barrier = pltpu.get_barrier_semaphore()
    peers = [{"seq": right}, {"seq": left}]
    peers += [{"head": lax.rem(x + k, nx)} for k in range(1, nx)]
    peers += [{"section": other, "head": lax.rem(x + k, nx)} for k in range(nx)]
    for peer in peers:
        pl.semaphore_signal(barrier, inc=1, device_id=peer, device_id_type=MESH)
    pl.semaphore_wait(barrier, len(peers))

    def scatter_copy(h, owner, source):
        return pltpu.make_async_remote_copy(
            src_ref=part.at[h, owner], dst_ref=headsum.at[h, source],
            send_sem=rs_send.at[h, owner], recv_sem=rs_recv.at[h, source],
            device_id={"section": other, "head": owner}, device_id_type=MESH,
        )

    def normed_copy(to, source):
        return pltpu.make_async_remote_copy(
            src_ref=normed.at[source], dst_ref=normed.at[source],
            send_sem=ag_send.at[to], recv_sem=ag_recv.at[source],
            device_id={"head": to}, device_id_type=MESH,
        )

    def half_copy():
        return pltpu.make_async_remote_copy(
            src_ref=xkeep.at[0], dst_ref=xhalf, send_sem=half_send, recv_sem=half_recv,
            device_id={"section": other}, device_id_type=MESH,
        )

    loads[0].wait()

    @pl.when(sec == 0)
    def _():
        for b in range(groups):
            n = rms_scale(hid[b].astype(jnp.float32), gain[...]).astype(jnp.bfloat16)
            for o in range(nx):
                normed[o, b * share:(b + 1) * share] = n[o * share:(o + 1) * share]

    @pl.when(sec == 1)
    def _():
        for h in range(2):
            for s in range(nx):
                scatter_copy(h, s, s).wait_recv()
        for b in range(groups):
            at = pl.ds(b * share, share)
            own = hid[b, pl.ds(pl.multiple_of(x * share, share), share)].astype(jnp.float32)
            halves = []
            for h in range(2):
                summed = own[:, h * half:(h + 1) * half]
                add = headsum[h, 0, at].astype(jnp.float32)
                for s in range(1, nx):
                    add = add + headsum[h, s, at].astype(jnp.float32)
                halves.append(summed + add)
                xkeep[h, at] = halves[h]
            n = rms_scale(jnp.concatenate(halves, axis=1), gain[...])
            normed[x, at] = n.astype(jnp.bfloat16)
        for k in range(1, nx):
            normed_copy(lax.rem(x + k, nx), x).start()
        half_copy().start()
        for k in range(1, nx):
            normed_copy(x, lax.rem(x + k, nx)).wait_recv()

    def by_block(values, store):
        for o in range(nx):
            for b in range(groups):
                store(b, o, values[(o * groups + b) * share:(o * groups + b + 1) * share])

    flat = normed[...].reshape(nx * mine, width)
    loads[1].wait()
    latent_full = rms_scale(dot(flat, wl[...]), lgain[...])

    def store_latent(b, o, v):
        lat[0, b, o * share:(o + 1) * share] = v
        kv[z, b * rows + o * share:b * rows + (o + 1) * share] = v.astype(jnp.bfloat16)

    by_block(latent_full, store_latent)

    def ring_copy(tile, chunk, step, to, send, recv):
        at = pl.ds(chunk * rows, rows)
        return pltpu.make_async_remote_copy(
            src_ref=kv.at[tile, at], dst_ref=kv.at[tile, at],
            send_sem=send.at[step, chunk], recv_sem=recv.at[step, chunk],
            device_id={"seq": to}, device_id_type=MESH,
        )

    def to_right(tile, chunk, step):
        return ring_copy(tile, chunk, step, right, r_send, r_recv)

    def to_left(tile, chunk, step):
        return ring_copy(tile, chunk, step, left, l_send, l_recv)

    far_right = groups - groups // 2

    for c in range(groups):
        to_right(z, c, 0).start()
        to_left(z, c, 0).start()

    loads[2].wait()
    loads[3].wait()
    query = dot(normed[...].reshape(nx * mine, width), wq[...]).astype(jnp.bfloat16)
    for h in range(heads):
        cols = slice(h * HD, (h + 1) * HD)
        a = (dot_t(query[:, cols], wk[:, cols]) * (1.0 / HD**0.5)).astype(jnp.bfloat16)

        def store_absorbed(b, o, v):
            absorbed[b, h * rows + o * share:h * rows + (o + 1) * share] = v

        by_block(a, store_absorbed)

    def attend(tiles, first):
        for qb in range(groups):
            n = (qb + 1) * rows
            q = absorbed[qb]
            keys = jnp.concatenate([kv[t, :n] for t in tiles], axis=0) if len(tiles) > 1 else kv[tiles[0], :n]
            lane = lax.broadcasted_iota(jnp.int32, (1, n * len(tiles)), 1)
            at = lane % n
            tile = jnp.full_like(lane, tiles[0])
            for i, t in enumerate(tiles[1:]):
                tile = jnp.where(lane >= (i + 1) * n, t, tile)
            pos = tile * rows + at % rows
            limit = jnp.full_like(lane, lengths[0])
            for b in range(1, qb):
                limit = jnp.where(at >= b * rows, lengths[b], limit)
            key_at = jnp.where(at >= qb * rows, pos, jnp.where(pos < limit, -1, FAR))
            row_at = z * rows + lax.broadcasted_iota(jnp.int32, (hrows, 1), 0) % rows
            scores = jnp.where(key_at <= row_at, dot_t(q, keys), NEG)
            peak = jnp.max(scores, axis=1, keepdims=True)
            if first:
                weights = jnp.exp(scores - peak)
                total[qb] = jnp.sum(weights, axis=1, keepdims=True)
                accum[qb] = dot(weights.astype(jnp.bfloat16), keys)
                top[qb] = peak
            else:
                old = top[qb]
                peak = jnp.maximum(old, peak)
                shrink = jnp.exp(old - peak)
                weights = jnp.exp(scores - peak)
                total[qb] = total[qb] * shrink + jnp.sum(weights, axis=1, keepdims=True)
                accum[qb] = accum[qb] * shrink + dot(weights.astype(jnp.bfloat16), keys)
                top[qb] = peak

    attend([z], True)

    def ring_step(step, carry):
        from_left = lax.rem(z - step + nz, nz)
        from_right = lax.rem(z + step, nz)
        for c in range(groups):
            to_right(from_left, c, step - 1).wait_recv()

            @pl.when(jnp.logical_or(step < mid - 1, c < far_right))
            def _():
                to_right(from_left, c, step).start()

            to_left(from_right, c, step - 1).wait_recv()

            @pl.when(jnp.logical_or(step < mid - 1, c >= far_right))
            def _():
                to_left(from_right, c, step).start()

        attend([from_left, from_right], False)
        return carry

    lax.fori_loop(1, mid, ring_step, 0)
    last = lax.rem(z + mid, nz)
    for c in range(groups):
        (to_right if c < far_right else to_left)(last, c, mid - 1).wait_recv()
    attend([last], False)

    loads[4].wait()
    loads[5].wait()
    for h in range(heads):
        at = slice(h * rows, (h + 1) * rows)
        context = jnp.concatenate(
            [(accum[b, at] / total[b, at]).astype(jnp.bfloat16) for b in range(groups)], axis=0
        )
        cols = slice(h * HD, (h + 1) * HD)
        attn[:, cols] = dot(context, wv[:, cols]).astype(jnp.bfloat16)

    def finish_copy(h, owner, source):
        return pltpu.make_async_remote_copy(
            src_ref=part.at[h, owner], dst_ref=finsum.at[source],
            send_sem=fin_send.at[h, owner], recv_sem=fin_recv.at[source],
            device_id={"section": h, "head": owner}, device_id_type=MESH,
        )

    for h in range(2):
        out = dot(attn[...], wo[:, h * half:(h + 1) * half]).astype(jnp.bfloat16)
        for b in range(groups):
            for o in range(nx):
                part[h, o, b * share:(b + 1) * share] = out[b * rows + o * share:b * rows + (o + 1) * share]

        @pl.when(sec == 0)
        def _():
            for k in range(nx):
                scatter_copy(h, lax.rem(x + nx - 1 - k, nx), x).start()

        @pl.when(sec == 1)
        def _():
            for k in range(1 if h == 1 else 0, nx):
                finish_copy(h, lax.rem(x + k, nx), x).start()

    @pl.when(sec == 0)
    def _():
        half_copy().wait_recv()
        for s in range(nx):
            finish_copy(0, x, s).wait_recv()

    @pl.when(sec == 1)
    def _():
        finsum[x] = part[1, x]
        xhalf[...] = xkeep[1]
        for k in range(1, nx):
            finish_copy(1, x, lax.rem(x + k, nx)).wait_recv()

    for b in range(groups):
        at = pl.ds(b * share, share)
        add = finsum[0, at].astype(jnp.float32)
        for s in range(1, nx):
            add = add + finsum[s, at].astype(jnp.float32)
        final[b] = xhalf[at] + add

    @pl.when(sec == 0)
    def _():
        for h in range(2):
            for o in range(nx):
                scatter_copy(h, o, x).wait_send()

    @pl.when(sec == 1)
    def _():
        half_copy().wait_send()
        for k in range(1, nx):
            normed_copy(lax.rem(x + k, nx), x).wait_send()
        for h in range(2):
            for k in range(1 if h == 1 else 0, nx):
                finish_copy(h, lax.rem(x + k, nx), x).wait_send()

    def drain(step, carry):
        for c in range(groups):

            @pl.when(jnp.logical_or(step < mid - 1, c < far_right))
            def _():
                to_right(z, c, step).wait_send()

            @pl.when(jnp.logical_or(step < mid - 1, c >= far_right))
            def _():
                to_left(z, c, step).wait_send()

        return carry

    lax.fori_loop(0, mid, drain, 0)


def shards(nz, nx, hidden, lengths, attn_gain, w_query, w_latent, latent_gain, w_key, w_value, w_out):
    groups, rows, width = hidden.shape
    rank = w_latent.shape[2]
    cols = w_key.shape[2]
    heads = cols // HD
    share = rows // nx
    mine = groups * share
    half = width // 2
    mid = nz // 2
    vmem, dma = pltpu.VMEM, pltpu.SemaphoreType.DMA
    whole = pl.BlockSpec(memory_space=pltpu.VMEM)
    hbm = pl.BlockSpec(memory_space=pl.ANY)
    bf16, f32 = jnp.bfloat16, jnp.float32
    final, lat = pl.pallas_call(
        functools.partial(kernel, nz, nx),
        out_shape=(
            jax.ShapeDtypeStruct((groups, share, half), f32),
            jax.ShapeDtypeStruct((1, groups, rows, rank), f32),
        ),
        in_specs=[pl.BlockSpec(memory_space=pltpu.SMEM), hbm, whole, hbm, hbm, whole, hbm, hbm, hbm],
        out_specs=(whole, whole),
        scratch_shapes=[
            vmem((groups, rows, width), bf16),
            vmem((width, cols), bf16),
            vmem((width, rank), bf16),
            vmem((rank, cols), bf16),
            vmem((rank, cols), bf16),
            vmem((cols, width), bf16),
            vmem((nx, mine, width), bf16),
            vmem((nz, groups * rows, rank), bf16),
            vmem((groups, heads * rows, rank), bf16),
            vmem((groups, heads * rows, 1), f32),
            vmem((groups, heads * rows, 1), f32),
            vmem((groups, heads * rows, rank), f32),
            vmem((groups * rows, cols), bf16),
            vmem((2, nx, mine, half), bf16),
            vmem((2, nx, mine, half), bf16),
            vmem((2, mine, half), f32),
            vmem((mine, half), f32),
            vmem((nx, mine, half), bf16),
            dma((6,)),
            dma((mid, groups)),
            dma((mid, groups)),
            dma((mid, groups)),
            dma((mid, groups)),
            dma((2, nx)),
            dma((2, nx)),
            dma((nx,)),
            dma((nx,)),
            dma,
            dma,
            dma((2, nx)),
            dma((nx,)),
        ],
        compiler_params=pltpu.CompilerParams(
            collective_id=0, has_side_effects=True, vmem_limit_bytes=48 * 1024 * 1024
        ),
    )(lengths, hidden, attn_gain, w_query, w_latent, latent_gain, w_key, w_value, w_out)
    seq_id, head_id = lax.axis_index("seq"), lax.axis_index("head")
    pos = seq_id * rows + jnp.arange(rows, dtype=jnp.int32)
    live = pos[None, :] < lengths[:, None]
    out_pos = seq_id * rows + head_id * share + jnp.arange(share, dtype=jnp.int32)
    live_out = out_pos[None, :] < lengths[:, None]
    final = jnp.where(live_out[:, :, None], final, 0.0)
    lat = jnp.where(live[None, :, :, None], lat, 0.0)
    return (final, lat)


def solution(mesh):
    return jax.shard_map(
        functools.partial(shards, mesh.shape["seq"], mesh.shape["head"]),
        mesh=mesh,
        in_specs=(
            P("rep", "seq", None),
            P("rep"),
            P("section", None),
            P("section", None, "head"),
            P("section", None, None),
            P("section", None),
            P("section", None, "head"),
            P("section", None, "head"),
            P("section", "head", None),
        ),
        out_specs=(P("rep", ("seq", "head"), "section"), P("section", "rep", "seq", None)),
        check_vma=False,
    )
```

time: 417 us -> 121 us (0.29)
  waiting for transfers between devices: 178 us -> 0 us
  Pallas kernels: 0 us -> 110 us
  starting transfers between devices: 67.4 us -> 0 us
  matrix products: 48.2 us -> 0 us
  blocking collectives: 47.5 us -> 0 us
  other arithmetic: 50.4 us -> 3.06 us
  local copies, waits for them, and re-layouts: 22.7 us -> 6.84 us
    all_to_all x5 -> x0, waiting for transfers between devices: 156 us -> none  [from_everyone(): return lax.all_to_all(copies, axis, split_axis=0, concat_axis=0, tiled=True)]
    pallas_call x0 -> x1, Pallas kernels: none -> 110 us  [shards(): pl.pallas_call(functools.partial(kernel, nz, nx), out_shape=(jax.ShapeDty...]
    all_to_all x5 -> x0, starting transfers between devices: 63.5 us -> none  [from_everyone(): return lax.all_to_all(copies, axis, split_axis=0, concat_axis=0, tiled=True)]
    dot_general x20 -> x0, matrix products: 48.2 us -> none  [the longest x4 17.6 us: shards(): jnp.einsum('hqr,ckr->hqck', absorbed, piece, preferred_element_type=jnp.f...]
    all_to_all x3 -> x0, blocking collectives: 40.4 us -> none  [from_everyone(): return lax.all_to_all(copies, axis, split_axis=0, concat_axis=0, tiled=True)]
    scatter x11 -> x0, other arithmetic: 22.8 us -> none  [the longest x3 10.3 us: shards(): full_cache.at[0, group_at].set(jnp.where(active, gathered, current))]
    ppermute x3 -> x0, waiting for transfers between devices: 22.4 us -> none  [shifted(): return lax.ppermute(value, axis, pairs)]
    reduce_sum x12 -> x0, other arithmetic: 13.7 us -> none  [the longest x4 9.92 us: online_step(): total = jnp.sum(weights, axis=(2, 3))]
  transfers between devices with their start and end apart: 8 -> 0, of which waited for: 8 -> 0; matrix products, arithmetic and copies ran while one was open for 9% -> 0% of each run, Pallas kernels for 0% -> 0%
where the time goes in v1:
time: 121 us
  Pallas kernels  110 us (91%)
  local copies, waits for them, and re-layouts  6.84 us (6%)
  other arithmetic  3.06 us (3%)
    pallas_call x1, Pallas kernels, shards(): pl.pallas_call(functools.partial(kernel, nz, nx), out_shape=(jax.ShapeDty...  110 us
    unnamed x14, local copies, waits for them, and re-layouts  6.84 us

profile of v1, /device:TPU:33, one launch (start us, length us, event | category | flops | bytes accessed | tf_op | source)
XLA Modules:
  0.0 120.9 jit_solution(9432018830747129742)
XLA Ops:
  0.6 0.7 broadcast_compare_fusion
  1.4 0.7 broadcast_compare_fusion.1
  2.1 0.0 copy-start
  2.1 1.6 %copy-done = bf16[1,2048,512]{2,1,0:T(8,128)(2,1)S(1)} copy-done((bf16[1,2048,512]{2,1,0:T(8,128)(2,1)S(1)}, bf16[1,2048,512]{2,1,0:T(8,128)(2,1)}, u32[]{:S(2)}) %copy-start) | copy-done | bytes 2097176
  3.7 0.0 copy-start.1
  3.7 1.1 copy-done.1
  4.8 0.0 copy-start.2
  4.8 1.0 copy-done.2
  5.9 0.0 copy-start.3
  5.9 1.0 copy-done.3
  6.9 0.0 copy-start.4
  6.9 0.7 copy-done.4
  7.6 0.0 copy-start.5
  7.6 0.7 copy-done.5
  8.3 0.0 copy-start.6
  8.3 0.7 copy-done.6
  9.0 110.3 %shard_map.104 = (f32[3,16,1024]{2,1,0:T(8,128)S(1)}, f32[1,3,64,512]{3,2,1,0:T(8,128)S(1)}) custom-call(s32[3]{0:T(128)S(1)} %copy-done.6, bf16[3,64,2048]{2,1,0:T(8,128)(2,1)S(1)} %copy-done.1, f32[1,2048]{1,0:T(1,128)S(1)} %copy-done.4, bf16[1,2048,512]{2,1,0:T(8,128)(2,1)S(1)} %copy-done, bf16[1,2048,512]{2,1,0:T(8,128)(2,1)} %wl_hbm.1, ...), custom_call_target="tpu_custom_call" | custom-call | tf_op jit(solution)/shard_map/pallas_call | solution.py:322
  119.3 0.8 broadcast_select_fusion.1
  120.0 0.8 broadcast_select_fusion
  (2 shorter events, 0.0 us)
Async XLA Ops:
  2.1 1.6 %copy-start = (bf16[1,2048,512]{2,1,0:T(8,128)(2,1)S(1)}, bf16[1,2048,512]{2,1,0:T(8,128)(2,1)}, u32[]{:S(2)}) copy-start(bf16[1,2048,512]{2,1,0:T(8,128)(2,1)} %wq_hbm.1) | copy-start | bytes 6291460
  3.7 1.1 copy-start.1
  4.8 1.0 copy-start.2
  5.9 1.0 copy-start.3
  6.9 0.7 copy-start.4
  7.6 0.7 copy-start.5
  8.3 0.7 copy-start.6

commit v2 on v1

v2 whole, which is shorter than its diff:
```python
import functools

import jax
import jax.numpy as jnp
from jax import lax
from jax.experimental import pallas as pl
from jax.experimental.pallas import tpu as pltpu
from jax.sharding import PartitionSpec as P

HD = 128
EPS = 1e-06
NEG = -1e30
MESH = pl.DeviceIdType.MESH
LAST = (((1,), (1,)), ((), ()))


def rms_scale(values, gain):
    mean_sq = jnp.mean(values * values, axis=-1, keepdims=True)
    return values * lax.rsqrt(mean_sq + EPS) * gain


def dot(a, b):
    return jnp.dot(a, b, preferred_element_type=jnp.float32)


def dot_t(a, b):
    return lax.dot_general(a, b, LAST, preferred_element_type=jnp.float32)


def kernel(
    nz, nx, len_hbm, hid_hbm, gain_hbm, wq_hbm, wl_hbm, lgain_hbm, wk_hbm, wv_hbm, wo_hbm,
    final, lat, lengths, hid, gain, lgain, wq, wl, wk, wv, wo, normed, kv, ownlat, absorbed, turned,
    top, total, accum, attn, part, headsum, xkeep, xhalf, finsum, load_sem,
    r_send, r_recv, l_send, l_recv, xa_send, xa_recv, xb_send, xb_recv, seed_send, seed_recv,
    rs_send, rs_recv, ag_send, ag_recv, half_send, half_recv, fin_send, fin_recv,
):
    z, x, sec = lax.axis_index("seq"), lax.axis_index("head"), lax.axis_index("section")
    other = 1 - sec
    x_up, x_down = lax.rem(x + 1, nx), lax.rem(x + nx - 1, nx)
    groups, rows, width = hid.shape
    rank = wl.shape[1]
    heads = wk.shape[1] // HD
    share = rows // nx
    mine = groups * share
    half = width // 2
    mid = nz // 2
    levels = mid // 2
    hrows = heads * rows

    loads = [
        pltpu.make_async_copy(src, dst, load_sem.at[i])
        for i, (src, dst) in enumerate(
            [
                (hid_hbm, hid), (gain_hbm, gain), (wl_hbm.at[0], wl), (lgain_hbm, lgain), (len_hbm, lengths),
                (wq_hbm.at[0], wq), (wk_hbm.at[0], wk), (wv_hbm.at[0], wv), (wo_hbm.at[0], wo),
            ]
        )
    ]
    for load in loads:
        load.start()

    barrier = pltpu.get_barrier_semaphore()
    peers = [{"seq": lax.rem(z + k, nz)} for k in (1, 2, nz - 2, nz - 1)]
    peers += [{"head": lax.rem(x + k, nx)} for k in range(1, nx)]
    peers += [{"section": other, "head": lax.rem(x + k, nx)} for k in range(nx)]
    for peer in peers:
        pl.semaphore_signal(barrier, inc=1, device_id=peer, device_id_type=MESH)

    def remote(src, dst, send, recv, to):
        return pltpu.make_async_remote_copy(
            src_ref=src, dst_ref=dst, send_sem=send, recv_sem=recv, device_id=to, device_id_type=MESH
        )

    def scatter_copy(h, owner, source):
        return remote(
            part.at[h, owner], headsum.at[h, source], rs_send.at[h, owner], rs_recv.at[h, source],
            {"section": other, "head": owner},
        )

    def normed_copy(to, source):
        return remote(normed.at[source], normed.at[source], ag_send.at[to], ag_recv.at[source], {"head": to})

    def half_copy():
        return remote(xkeep.at[0], xhalf, half_send, half_recv, {"section": other})

    def seed_copy(quarter):
        return remote(kv.at[z, quarter], kv.at[z, quarter], seed_send, seed_recv, {"head": x_down})

    def right_copy(d, hop, q):
        spot = kv.at[lax.rem(z + nz + hop - d, nz), lax.rem(x + q, nx)]
        return remote(spot, spot, r_send.at[d - 1, q], r_recv.at[d - 1, q], {"seq": lax.rem(z + hop, nz)})

    def left_copy(d, hop, q):
        spot = kv.at[lax.rem(z + nz - hop + d, nz), lax.rem(x + q, nx)]
        return remote(spot, spot, l_send.at[d - 1, q], l_recv.at[d - 1, q], {"seq": lax.rem(z + nz - hop, nz)})

    def up_copy(tile, slot, quarter):
        spot = kv.at[tile, quarter]
        return remote(spot, spot, xa_send.at[slot], xa_recv.at[slot], {"head": x_up})

    def down_copy(tile, slot, quarter):
        spot = kv.at[tile, quarter]
        return remote(spot, spot, xb_send.at[slot], xb_recv.at[slot], {"head": x_down})

    def across(tile, slot, q):
        if q == 0:
            up_copy(tile, slot, x).start()
        else:
            down_copy(tile, slot, x_up).start()

    def await_across(tile, slot):
        up_copy(tile, slot, x_down).wait_recv()
        down_copy(tile, slot, lax.rem(x + 2, nx)).wait_recv()

    def pieces(values):
        for o in range(nx):
            for b in range(groups):
                yield b, o, values[(o * groups + b) * share:(o * groups + b + 1) * share]

    def latents():
        flat = normed[...].reshape(nx * mine, width)
        full = rms_scale(dot(flat, wl[...]), lgain[...])
        for b, o, v in pieces(full):
            pos = z * rows + o * share + lax.broadcasted_iota(jnp.int32, (share, 1), 0)
            lat[0, b, o * share:(o + 1) * share] = jnp.where(pos < lengths[b], v, 0.0)
        return full.astype(jnp.bfloat16).reshape(nx, mine, rank)

    loads[0].wait()
    loads[1].wait()

    @pl.when(sec == 0)
    def _():
        for b in range(groups):
            n = rms_scale(hid[b].astype(jnp.float32), gain[...]).astype(jnp.bfloat16)
            for o in range(nx):
                normed[o, b * share:(b + 1) * share] = n[o * share:(o + 1) * share]

    for load in loads[2:5]:
        load.wait()

    @pl.when(sec == 0)
    def _():
        kv[z] = latents()

    with jax.named_scope("barrier"):
        pl.semaphore_wait(barrier, len(peers))

    @pl.when(sec == 1)
    def _():
        with jax.named_scope("rswait"):
            for h in range(2):
                for s in range(nx):
                    scatter_copy(h, s, s).wait_recv()
        for b in range(groups):
            at = pl.ds(b * share, share)
            own = hid[b, pl.ds(pl.multiple_of(x * share, share), share)].astype(jnp.float32)
            halves = []
            for h in range(2):
                add = headsum[h, 0, at].astype(jnp.float32)
                for s in range(1, nx):
                    add = add + headsum[h, s, at].astype(jnp.float32)
                halves.append(own[:, h * half:(h + 1) * half] + add)
                xkeep[h, at] = halves[h]
            n = rms_scale(jnp.concatenate(halves, axis=1), gain[...])
            normed[x, at] = n.astype(jnp.bfloat16)
        early = rms_scale(dot(normed[x], wl[...]), lgain[...])
        kv[z, x] = early.astype(jnp.bfloat16)
        seed_copy(x).start()

    def first_sends(q):
        for hop in (1, 2):
            right_copy(hop, hop, q).start()
            left_copy(hop, hop, q).start()

    first_sends(0)

    @pl.when(sec == 1)
    def _():
        for k in range(1, nx):
            normed_copy(lax.rem(x + k, nx), x).start()
        half_copy().start()
        with jax.named_scope("seedwait"):
            seed_copy(x_up).wait_recv()

    first_sends(1)

    @pl.when(sec == 1)
    def _():
        with jax.named_scope("agwait"):
            for k in range(1, nx):
                normed_copy(x, lax.rem(x + k, nx)).wait_recv()
        ownlat[...] = latents()
        for k in range(2, nx):
            o = lax.rem(x + k, nx)
            kv[z, o] = ownlat[o]

    loads[5].wait()
    loads[6].wait()
    with jax.named_scope("query"):
        query = dot(normed[...].reshape(nx * mine, width), wq[...]).astype(jnp.bfloat16)
        for h in range(heads):
            cols = slice(h * HD, (h + 1) * HD)
            a = (dot_t(query[:, cols], wk[:, cols]) * (1.0 / HD**0.5)).astype(jnp.bfloat16)
            for b, o, v in pieces(a):
                absorbed[b, h * rows + o * share:h * rows + (o + 1) * share] = v
        for b in range(groups):
            turned[b] = absorbed[b].T

    key_at = lax.broadcasted_iota(jnp.int32, (rows, hrows), 0)
    row_at = lax.broadcasted_iota(jnp.int32, (rows, hrows), 1) % rows

    def attend(tiles, own):
        keys, keep = [], {}
        for b in range(groups):
            for t in tiles:
                keys.append(kv[t, :, b * share:(b + 1) * share].reshape(rows, rank))
        keys = jnp.concatenate(keys, axis=0)
        keys_t = keys.T
        each = rows * len(tiles)

        def scores_of(qb):
            return dot(keys[:(qb + 1) * each], turned[qb])

        def fold(qb, scores):
            parts = []
            for b in range(qb + 1):
                for i, t in enumerate(tiles):
                    start = b * each + i * rows
                    s = scores[start:start + rows]
                    if b < qb:
                        seen = key_at < lengths[b] - t * rows
                    elif own:
                        seen = key_at <= row_at
                    else:
                        seen = key_at < jnp.where(t < z, rows, 0)
                    parts.append(jnp.where(seen, s, NEG))
            scores = jnp.concatenate(parts, axis=0)
            peak = jnp.max(scores, axis=0, keepdims=True)
            if not own:
                old = top[qb]
                peak = jnp.maximum(old, peak)
                shrink = jnp.exp(old - peak)
            weights = jnp.exp(scores - peak)
            add = jnp.sum(weights, axis=0, keepdims=True)
            gained = dot(keys_t[:, :(qb + 1) * each], weights.astype(jnp.bfloat16))
            if own:
                total[qb] = add
                accum[qb] = gained
            else:
                total[qb] = total[qb] * shrink + add
                accum[qb] = accum[qb] * shrink + gained
            top[qb] = peak

        ahead = scores_of(0)
        for qb in range(groups):
            now = ahead
            if qb + 1 < groups:
                ahead = scores_of(qb + 1)
            fold(qb, now)

    with jax.named_scope("attend_own"):
        attend([z], True)

    def tile_left(d):
        return lax.rem(z + nz - d, nz)

    def tile_right(d):
        return lax.rem(z + d, nz)

    def level(k, carry):
        near, deep = 2 * k + 1, 2 * k + 2

        @pl.when(k < levels)
        def _():
            with jax.named_scope("zwait"):
                for q in range(2):
                    right_copy(deep, 0, q).wait_recv()

                    @pl.when(k < levels - 1)
                    def _():
                        right_copy(deep + 1, 1, q).start()
                        right_copy(deep + 2, 2, q).start()

                    across(tile_left(deep), deep - 1, q)

                    @pl.when(k < levels - 1)
                    def _():
                        left_copy(deep, 0, q).wait_recv()
                        left_copy(deep + 1, 1, q).start()

                        @pl.when(k < levels - 2)
                        def _():
                            left_copy(deep + 2, 2, q).start()

                        across(tile_right(deep), mid + deep - 1, q)

                for q in range(2):
                    right_copy(near, 0, q).wait_recv()
                    across(tile_left(near), near - 1, q)
                    left_copy(near, 0, q).wait_recv()
                    across(tile_right(near), mid + near - 1, q)

        def pair(d, c):
            with jax.named_scope("xwait"):
                await_across(tile_left(d), d - 1)
                await_across(tile_right(d), mid + d - 1)
            with jax.named_scope("attend_pair"):
                attend([tile_left(d), tile_right(d)], False)
            return c

        lax.fori_loop(jnp.maximum(1, 2 * k - 1), jnp.minimum(2 * k, mid - 1) + 1, pair, 0)
        return carry

    lax.fori_loop(0, levels + 1, level, 0)
    with jax.named_scope("farwait"):
        await_across(tile_left(mid), mid - 1)
    with jax.named_scope("attend_far"):
        attend([tile_left(mid)], False)

    loads[7].wait()
    loads[8].wait()
    with jax.named_scope("value"):
        context = [(accum[b] / total[b]).astype(jnp.bfloat16).T for b in range(groups)]
        for h in range(heads):
            rows_h = jnp.concatenate([c[h * rows:(h + 1) * rows] for c in context], axis=0)
            cols = slice(h * HD, (h + 1) * HD)
            attn[:, cols] = dot(rows_h, wv[:, cols]).astype(jnp.bfloat16)

    def finish_copy(h, owner, source):
        return remote(
            part.at[h, owner], finsum.at[source], fin_send.at[h, owner], fin_recv.at[source],
            {"section": h, "head": owner},
        )

    for h in range(2):
        out = dot(attn[...], wo[:, h * half:(h + 1) * half]).astype(jnp.bfloat16)
        for b in range(groups):
            for o in range(nx):
                part[h, o, b * share:(b + 1) * share] = out[b * rows + o * share:b * rows + (o + 1) * share]

        @pl.when(sec == 0)
        def _():
            for k in range(nx):
                scatter_copy(h, lax.rem(x + nx - 1 - k, nx), x).start()

        @pl.when(sec == 1)
        def _():
            for k in range(1 if h == 1 else 0, nx):
                finish_copy(h, lax.rem(x + k, nx), x).start()

    @pl.when(sec == 0)
    def _():
        with jax.named_scope("finwait0"):
            half_copy().wait_recv()
            for s in range(nx):
                finish_copy(0, x, s).wait_recv()

    @pl.when(sec == 1)
    def _():
        finsum[x] = part[1, x]
        xhalf[...] = xkeep[1]
        with jax.named_scope("finwait1"):
            for k in range(1, nx):
                finish_copy(1, x, lax.rem(x + k, nx)).wait_recv()

    for b in range(groups):
        at = pl.ds(b * share, share)
        add = finsum[0, at].astype(jnp.float32)
        for s in range(1, nx):
            add = add + finsum[s, at].astype(jnp.float32)
        pos = z * rows + x * share + lax.broadcasted_iota(jnp.int32, (share, 1), 0)
        final[b] = jnp.where(pos < lengths[b], xhalf[at] + add, 0.0)

    @pl.when(sec == 0)
    def _():
        for h in range(2):
            for o in range(nx):
                scatter_copy(h, o, x).wait_send()

    @pl.when(sec == 1)
    def _():
        half_copy().wait_send()
        seed_copy(x).wait_send()
        for k in range(1, nx):
            normed_copy(lax.rem(x + k, nx), x).wait_send()
        for h in range(2):
            for k in range(1 if h == 1 else 0, nx):
                finish_copy(h, lax.rem(x + k, nx), x).wait_send()

    def drain(d, carry):
        for q in range(2):
            right_copy(d, 1, q).wait_send()

        up_copy(z, d - 1, x).wait_send()
        down_copy(z, d - 1, x).wait_send()

        @pl.when(d < mid)
        def _():
            for q in range(2):
                left_copy(d, 1, q).wait_send()

            up_copy(z, mid + d - 1, x).wait_send()
            down_copy(z, mid + d - 1, x).wait_send()

        return carry

    with jax.named_scope("drain"):
        lax.fori_loop(1, mid + 1, drain, 0)


def shards(nz, nx, hidden, lengths, attn_gain, w_query, w_latent, latent_gain, w_key, w_value, w_out):
    groups, rows, width = hidden.shape
    rank = w_latent.shape[2]
    cols = w_key.shape[2]
    heads = cols // HD
    share = rows // nx
    mine = groups * share
    half = width // 2
    mid = nz // 2
    vmem, dma = pltpu.VMEM, pltpu.SemaphoreType.DMA
    whole = pl.BlockSpec(memory_space=pltpu.VMEM)
    hbm = pl.BlockSpec(memory_space=pl.ANY)
    bf16, f32 = jnp.bfloat16, jnp.float32
    return pl.pallas_call(
        functools.partial(kernel, nz, nx),
        out_shape=(
            jax.ShapeDtypeStruct((groups, share, half), f32),
            jax.ShapeDtypeStruct((1, groups, rows, rank), f32),
        ),
        in_specs=[hbm] * 9,
        out_specs=(whole, whole),
        scratch_shapes=[
            pltpu.SMEM((groups,), jnp.int32),
            vmem((groups, rows, width), bf16),
            vmem((1, width), f32),
            vmem((1, rank), f32),
            vmem((width, cols), bf16),
            vmem((width, rank), bf16),
            vmem((rank, cols), bf16),
            vmem((rank, cols), bf16),
            vmem((cols, width), bf16),
            vmem((nx, mine, width), bf16),
            vmem((nz, nx, mine, rank), bf16),
            vmem((nx, mine, rank), bf16),
            vmem((groups, heads * rows, rank), bf16),
            vmem((groups, rank, heads * rows), bf16),
            vmem((groups, 1, heads * rows), f32),
            vmem((groups, 1, heads * rows), f32),
            vmem((groups, rank, heads * rows), f32),
            vmem((groups * rows, cols), bf16),
            vmem((2, nx, mine, half), bf16),
            vmem((2, nx, mine, half), bf16),
            vmem((2, mine, half), f32),
            vmem((mine, half), f32),
            vmem((nx, mine, half), bf16),
            dma((9,)),
            dma((mid, 2)),
            dma((mid, 2)),
            dma((mid, 2)),
            dma((mid, 2)),
            dma((nz - 1,)),
            dma((nz - 1,)),
            dma((nz - 1,)),
            dma((nz - 1,)),
            dma,
            dma,
            dma((2, nx)),
            dma((2, nx)),
            dma((nx,)),
            dma((nx,)),
            dma,
            dma,
            dma((2, nx)),
            dma((nx,)),
        ],
        compiler_params=pltpu.CompilerParams(
            collective_id=0, has_side_effects=True, vmem_limit_bytes=67043328
        ),
    )(lengths, hidden, attn_gain, w_query, w_latent, latent_gain, w_key, w_value, w_out)


def solution(mesh):
    return jax.shard_map(
        functools.partial(shards, mesh.shape["seq"], mesh.shape["head"]),
        mesh=mesh,
        in_specs=(
            P("rep", "seq", None),
            P("rep"),
            P("section", None),
            P("section", None, "head"),
            P("section", None, None),
            P("section", None),
            P("section", None, "head"),
            P("section", None, "head"),
            P("section", "head", None),
        ),
        out_specs=(P("rep", ("seq", "head"), "section"), P("section", "rep", "seq", None)),
        check_vma=False,
    )
```

time: 121 us -> 102 us (0.84)
  Pallas kernels: 110 us -> 97.6 us
  local copies, waits for them, and re-layouts: 6.84 us -> 3.38 us
  other arithmetic: 3.06 us -> 0 us
    pallas_call x1, Pallas kernels: 110 us -> 97.6 us  [shards(): pl.pallas_call(functools.partial(kernel, nz, nx), out_shape=(jax.ShapeDty...]
    unnamed x14 -> x2, local copies, waits for them, and re-layouts: 6.84 us -> 3.38 us
    select_n x2 -> x0, other arithmetic: 1.6 us -> none  [the longest x1 0.84 us: shards(): lat = jnp.where(live[None, :, :, None], lat, 0.0)]
    lt x2 -> x0, other arithmetic: 1.46 us -> none  [the longest x1 0.73 us: shards(): live = pos[None, :] < lengths[:, None]]
where the time goes in v2:
time: 102 us
  Pallas kernels  97.6 us (96%)
  local copies, waits for them, and re-layouts  3.38 us (3%)
    pallas_call x1, Pallas kernels, shards(): pl.pallas_call(functools.partial(kernel, nz, nx), out_shape=(jax.ShapeDty...  97.6 us
    unnamed x2, local copies, waits for them, and re-layouts  3.38 us

profile of v2, /device:TPU:33, one launch (start us, length us, event | category | flops | bytes accessed | tf_op | source)
XLA Modules:
  0.0 101.7 jit_solution(15173494663515062369)
XLA Ops:
  0.6 97.6 %shard_map.104 = (f32[3,16,1024]{2,1,0:T(8,128)}, f32[1,3,64,512]{3,2,1,0:T(8,128)}) custom-call(s32[3]{0:T(128)} %len_hbm.1, bf16[3,64,2048]{2,1,0:T(8,128)(2,1)} %hid_hbm.1, f32[1,2048]{1,0:T(1,128)} %gain_hbm.1, bf16[1,2048,512]{2,1,0:T(8,128)(2,1)} %wq_hbm.1, bf16[1,2048,512]{2,1,0:T(8,128)(2,1)} %wl_hbm.1, f32[1,512]{1,0:T(1,128)} %lgain_hbm.1, ...), custom_call_target="tpu_custom_call" | custom-call | tf_op jit(solution)/shard_map/pallas_call | solution.py:424
  98.3 1.6 %copy.13 = f32[3,16,1024]{2,1,0:T(8,128)} copy(f32[3,16,1024]{2,1,0:T(8,128)} %get-tuple-element.4) | data formatting | bytes 393216
  99.9 1.8 %copy.14 = f32[1,3,64,512]{3,2,1,0:T(8,128)} copy(f32[1,3,64,512]{3,2,1,0:T(8,128)} %get-tuple-element.5) | data formatting | bytes 786432

commit v3 on v2

v3 whole, which is shorter than its diff:
```python
import functools

import jax
import jax.numpy as jnp
from jax import lax
from jax.experimental import pallas as pl
from jax.experimental.pallas import tpu as pltpu
from jax.sharding import PartitionSpec as P

HD = 128
EPS = 1e-06
NEG = -1e30
MESH = pl.DeviceIdType.MESH
LAST = (((1,), (1,)), ((), ()))


def rms_scale(values, gain):
    mean_sq = jnp.mean(values * values, axis=-1, keepdims=True)
    return values * lax.rsqrt(mean_sq + EPS) * gain


def dot(a, b):
    return jnp.dot(a, b, preferred_element_type=jnp.float32)


def dot_t(a, b):
    return lax.dot_general(a, b, LAST, preferred_element_type=jnp.float32)


def kernel(
    nz, nx, len_hbm, hid_hbm, gain_hbm, wq_hbm, wl_hbm, lgain_hbm, wk_hbm, wv_hbm, wo_hbm,
    final, lat, lengths, hid, gain, lgain, wq, wl, wk, wv, wo, normed, kv, ownlat, absorbed, turned, last_keys, last_turned,
    top, total, accum, attn, part, headsum, xkeep, xhalf, finsum, load_sem,
    r_send, r_recv, l_send, l_recv, xa_send, xa_recv, xb_send, xb_recv, seed_send, seed_recv,
    rs_send, rs_recv, ag_send, ag_recv, half_send, half_recv, fin_send, fin_recv,
):
    z, x, sec = lax.axis_index("seq"), lax.axis_index("head"), lax.axis_index("section")
    other = 1 - sec
    x_up, x_down = lax.rem(x + 1, nx), lax.rem(x + nx - 1, nx)
    groups, rows, width = hid.shape
    rank = wl.shape[1]
    heads = wk.shape[1] // HD
    share = rows // nx
    mine = groups * share
    half = width // 2
    mid = nz // 2
    levels = mid // 2
    hrows = heads * rows

    loads = [
        pltpu.make_async_copy(src, dst, load_sem.at[i])
        for i, (src, dst) in enumerate(
            [
                (hid_hbm, hid), (gain_hbm, gain), (wl_hbm.at[0], wl), (lgain_hbm, lgain), (len_hbm, lengths),
                (wq_hbm.at[0], wq), (wk_hbm.at[0], wk), (wv_hbm.at[0], wv), (wo_hbm.at[0], wo),
            ]
        )
    ]
    for load in loads:
        load.start()

    main = mine - share
    for o in range(nx):
        kv[:, o, main:] = jnp.zeros((nz, share, rank), kv.dtype)

    barrier = pltpu.get_barrier_semaphore()
    peers = [{"seq": lax.rem(z + k, nz)} for k in (1, 2, nz - 2, nz - 1)]
    peers += [{"head": lax.rem(x + k, nx)} for k in range(1, nx)]
    peers += [{"section": other, "head": lax.rem(x + k, nx)} for k in range(nx)]
    for peer in peers:
        pl.semaphore_signal(barrier, inc=1, device_id=peer, device_id_type=MESH)

    def remote(src, dst, send, recv, to):
        return pltpu.make_async_remote_copy(
            src_ref=src, dst_ref=dst, send_sem=send, recv_sem=recv, device_id=to, device_id_type=MESH
        )

    def scatter_copy(b, owner, source):
        return remote(
            part.at[b, owner], headsum.at[source, b], rs_send.at[b, owner], rs_recv.at[b, source],
            {"section": other, "head": owner},
        )

    def normed_copy(to, source):
        return remote(normed.at[source], normed.at[source], ag_send.at[to], ag_recv.at[source], {"head": to})

    def half_copy():
        return remote(xkeep.at[0], xhalf, half_send, half_recv, {"section": other})

    def seed_copy(quarter):
        return remote(kv.at[z, quarter], kv.at[z, quarter], seed_send, seed_recv, {"head": x_down})

    def tile_left(d):
        return lax.rem(z + nz - d, nz)

    def tile_right(d):
        return lax.rem(z + d, nz)

    def either(carry, make, act):
        @pl.when(carry)
        def _():
            getattr(make(mine), act)()

        @pl.when(jnp.logical_not(carry))
        def _():
            getattr(make(main), act)()

    def right_copy(d, hop, q, act):
        tile = tile_left(d - hop)

        def make(count):
            spot = kv.at[tile, lax.rem(x + q, nx), pl.ds(0, count)]
            return remote(spot, spot, r_send.at[d - 1, q], r_recv.at[d - 1, q], {"seq": tile_right(hop)})

        either(tile + d < nz, make, act)

    def left_copy(d, hop, q, deep, act):
        tile = tile_right(d - hop)

        def make(count):
            spot = kv.at[tile, lax.rem(x + q, nx), pl.ds(0, count)]
            return remote(spot, spot, l_send.at[d - 1, q], l_recv.at[d - 1, q], {"seq": tile_left(hop)})

        either(tile < mid - 1 if deep else tile < d, make, act)

    def up_copy(tile, slot, quarter, act):
        def make(count):
            spot = kv.at[tile, quarter, pl.ds(0, count)]
            return remote(spot, spot, xa_send.at[slot], xa_recv.at[slot], {"head": x_up})

        either(tile <= z, make, act)

    def down_copy(tile, slot, quarter, act):
        def make(count):
            spot = kv.at[tile, quarter, pl.ds(0, count)]
            return remote(spot, spot, xb_send.at[slot], xb_recv.at[slot], {"head": x_down})

        either(tile <= z, make, act)

    def across(tile, slot, q):
        if q == 0:
            up_copy(tile, slot, x, "start")
        else:
            down_copy(tile, slot, x_up, "start")

    def await_across(tile, slot):
        up_copy(tile, slot, x_down, "wait_recv")
        down_copy(tile, slot, lax.rem(x + 2, nx), "wait_recv")

    def pieces(values):
        for o in range(nx):
            for b in range(groups):
                yield b, o, values[(o * groups + b) * share:(o * groups + b + 1) * share]

    def latents():
        flat = normed[...].reshape(nx * mine, width)
        full = rms_scale(dot(flat, wl[...]), lgain[...])
        for b, o, v in pieces(full):
            pos = z * rows + o * share + lax.broadcasted_iota(jnp.int32, (share, 1), 0)
            lat[0, b, o * share:(o + 1) * share] = jnp.where(pos < lengths[b], v, 0.0)
        return full.astype(jnp.bfloat16).reshape(nx, mine, rank)

    loads[0].wait()
    loads[1].wait()

    @pl.when(sec == 0)
    def _():
        for b in range(groups):
            n = rms_scale(hid[b].astype(jnp.float32), gain[...]).astype(jnp.bfloat16)
            for o in range(nx):
                normed[o, b * share:(b + 1) * share] = n[o * share:(o + 1) * share]

    for load in loads[2:5]:
        load.wait()

    @pl.when(sec == 0)
    def _():
        kv[z] = latents()

    with jax.named_scope("barrier"):
        pl.semaphore_wait(barrier, len(peers))

    @pl.when(sec == 1)
    def _():
        for b in range(groups):
            with jax.named_scope("rswait"):
                for k in range(nx):
                    scatter_copy(b, x, k).wait_recv()
            at = pl.ds(b * share, share)
            own = hid[b, pl.ds(pl.multiple_of(x * share, share), share)].astype(jnp.float32)
            halves = []
            for h in range(2):
                add = headsum[0, b, h].astype(jnp.float32)
                for k in range(1, nx):
                    add = add + headsum[k, b, h].astype(jnp.float32)
                halves.append(own[:, h * half:(h + 1) * half] + add)
                xkeep[h, at] = halves[h]
            n = rms_scale(jnp.concatenate(halves, axis=1), gain[...])
            normed[x, at] = n.astype(jnp.bfloat16)
        early = rms_scale(dot(normed[x], wl[...]), lgain[...])
        kv[z, x] = early.astype(jnp.bfloat16)
        seed_copy(x).start()

    def first_sends(q):
        for hop in (2, 1):
            right_copy(hop, hop, q, "start")
            left_copy(hop, hop, q, hop == 2, "start")

    first_sends(0)

    @pl.when(sec == 1)
    def _():
        for k in range(1, nx):
            normed_copy(lax.rem(x + k, nx), x).start()
        half_copy().start()
        with jax.named_scope("seedwait"):
            seed_copy(x_up).wait_recv()

    first_sends(1)

    def arrive(k):
        near, deep = 2 * k + 1, 2 * k + 2
        with jax.named_scope("zwait"):
            for q in range(2):
                right_copy(deep, 0, q, "wait_recv")

                @pl.when(k < levels - 1)
                def _():
                    right_copy(deep + 2, 2, q, "start")
                    left_copy(deep, 0, q, True, "wait_recv")

                @pl.when(k < levels - 2)
                def _():
                    left_copy(deep + 2, 2, q, True, "start")

            for q in range(2):

                @pl.when(k < levels - 1)
                def _():
                    right_copy(deep + 1, 1, q, "start")
                    left_copy(deep + 1, 1, q, False, "start")
                    across(tile_right(deep), mid + deep - 1, q)

                across(tile_left(deep), deep - 1, q)
            for q in range(2):
                right_copy(near, 0, q, "wait_recv")
                across(tile_left(near), near - 1, q)
                left_copy(near, 0, q, False, "wait_recv")
                across(tile_right(near), mid + near - 1, q)

    arrive(0)

    @pl.when(sec == 1)
    def _():
        with jax.named_scope("agwait"):
            for k in range(1, nx):
                normed_copy(x, lax.rem(x + k, nx)).wait_recv()
        ownlat[...] = latents()
        for k in range(2, nx):
            o = lax.rem(x + k, nx)
            kv[z, o] = ownlat[o]

    loads[5].wait()
    loads[6].wait()
    with jax.named_scope("query"):
        query = dot(normed[...].reshape(nx * mine, width), wq[...]).astype(jnp.bfloat16)
        for h in range(heads):
            cols = slice(h * HD, (h + 1) * HD)
            a = (dot_t(query[:, cols], wk[:, cols]) * (1.0 / HD**0.5)).astype(jnp.bfloat16)
            for b, o, v in pieces(a):
                absorbed[b, h * rows + o * share:h * rows + (o + 1) * share] = v
        for b in range(groups):
            turned[b] = absorbed[b].T

    key_at = lax.broadcasted_iota(jnp.int32, (rows, hrows), 0)
    row_at = lax.broadcasted_iota(jnp.int32, (rows, hrows), 1) % rows

    def gather_keys(tiles):
        keys = []
        for b in range(groups):
            for t in tiles:
                keys.append(kv[t, :, b * share:(b + 1) * share].reshape(rows, rank))
        keys = jnp.concatenate(keys, axis=0)
        return keys, keys.T

    def fold(qb, scores, keys_t, tiles, own, light):
        parts = []
        each = rows * len(tiles)
        blocks = qb if light else qb + 1
        for b in range(blocks):
            for i, t in enumerate(tiles):
                start = b * each + i * rows
                s = scores[start:start + rows]
                if b < qb:
                    seen = key_at < lengths[b] - t * rows
                elif own:
                    seen = key_at <= row_at
                else:
                    seen = key_at < jnp.where(t < z, rows, 0)
                parts.append(jnp.where(seen, s, NEG))
        scores = jnp.concatenate(parts, axis=0)
        peak = jnp.max(scores, axis=0, keepdims=True)
        if not own:
            old = top[qb]
            peak = jnp.maximum(old, peak)
            shrink = jnp.exp(old - peak)
        weights = jnp.exp(scores - peak)
        add = jnp.sum(weights, axis=0, keepdims=True)
        gained = dot(keys_t, weights.astype(jnp.bfloat16))
        if own:
            total[qb] = add
            accum[qb] = gained
        else:
            total[qb] = total[qb] * shrink + add
            accum[qb] = accum[qb] * shrink + gained
        top[qb] = peak

    def attend(tiles, own, light):
        keys, keys_t = gather_keys(tiles)
        each = rows * len(tiles)

        def count(qb):
            return (qb if light else qb + 1) * each

        start = 1 if light else 0
        ahead = dot(keys[:count(start)], turned[start])
        for qb in range(start, groups):
            now = ahead
            if qb + 1 < groups:
                ahead = dot(keys[:count(qb + 1)], turned[qb + 1])
            fold(qb, now, keys_t[:, :count(qb)], tiles, own, light)

    with jax.named_scope("attend_own"):
        attend([z], True, False)

    def level(k, carry):
        arrive(k)

        def pair(d, c):
            with jax.named_scope("xwait"):
                await_across(tile_left(d), d - 1)
                await_across(tile_right(d), mid + d - 1)
            light = jnp.logical_and(z < d, z + d < nz)

            @pl.when(light)
            def _():
                with jax.named_scope("attend_light"):
                    attend([tile_left(d), tile_right(d)], False, True)

            @pl.when(jnp.logical_not(light))
            def _():
                with jax.named_scope("attend_pair"):
                    attend([tile_left(d), tile_right(d)], False, False)

            return c

        lax.fori_loop(2 * k - 1, 2 * k + 1, pair, 0)
        return carry

    lax.fori_loop(1, levels, level, 0)
    ends = [tile_left(mid - 1), tile_right(mid - 1), tile_left(mid)]
    with jax.named_scope("farwait"):
        await_across(ends[0], mid - 2)
        await_across(ends[1], 2 * mid - 2)
        await_across(ends[2], mid - 1)
    end_keys, end_turned = gather_keys(ends)
    last_keys[...] = end_keys
    last_turned[...] = end_turned
    all_later = z < mid - 1

    for load in loads[7:]:
        load.wait()

    def finish_copy(b, h, owner, source):
        return remote(
            part.at[b, owner, h], finsum.at[source, b], fin_send.at[b, h, owner], fin_recv.at[b, source],
            {"section": h, "head": owner},
        )

    for b in range(groups):

        def last_fold(light):
            n = (b if light else b + 1) * len(ends) * rows
            fold(b, dot(last_keys[:n], turned[b]), last_turned[:, :n], ends, False, light)

        with jax.named_scope("attend_last"):
            if b > 0:

                @pl.when(all_later)
                def _():
                    last_fold(True)

            @pl.when(jnp.logical_not(all_later))
            def _():
                last_fold(False)

        with jax.named_scope("project"):
            context = (accum[b] / total[b]).astype(jnp.bfloat16).T
            for h in range(heads):
                cols = slice(h * HD, (h + 1) * HD)
                attn[:, cols] = dot(context[h * rows:(h + 1) * rows], wv[:, cols]).astype(jnp.bfloat16)
            for h in range(2):
                out = dot(attn[...], wo[:, h * half:(h + 1) * half]).astype(jnp.bfloat16)
                for o in range(nx):
                    part[b, o, h] = out[o * share:(o + 1) * share]

        @pl.when(sec == 0)
        def _():
            for k in range(nx):
                scatter_copy(b, lax.rem(x + nx - 1 - k, nx), x).start()

        @pl.when(sec == 1)
        def _():
            for k in range(1, nx):
                for h in range(2):
                    finish_copy(b, h, lax.rem(x + k, nx), x).start()
            finish_copy(b, 0, x, x).start()

    @pl.when(sec == 0)
    def _():
        half_copy().wait_recv()

    @pl.when(sec == 1)
    def _():
        xhalf[...] = xkeep[1]

    for b in range(groups):

        @pl.when(sec == 0)
        def _():
            with jax.named_scope("finwait0"):
                for k in range(nx):
                    finish_copy(b, 0, x, k).wait_recv()

        @pl.when(sec == 1)
        def _():
            finsum[x, b] = part[b, x, 1]
            with jax.named_scope("finwait1"):
                for k in range(1, nx):
                    finish_copy(b, 1, x, lax.rem(x + k, nx)).wait_recv()

        at = pl.ds(b * share, share)
        add = finsum[0, b].astype(jnp.float32)
        for k in range(1, nx):
            add = add + finsum[k, b].astype(jnp.float32)
        pos = z * rows + x * share + lax.broadcasted_iota(jnp.int32, (share, 1), 0)
        final[b] = jnp.where(pos < lengths[b], xhalf[at] + add, 0.0)

    @pl.when(sec == 0)
    def _():
        for b in range(groups):
            for o in range(nx):
                scatter_copy(b, o, x).wait_send()

    @pl.when(sec == 1)
    def _():
        half_copy().wait_send()
        seed_copy(x).wait_send()
        for k in range(1, nx):
            normed_copy(lax.rem(x + k, nx), x).wait_send()
        for b in range(groups):
            for k in range(1, nx):
                for h in range(2):
                    finish_copy(b, h, lax.rem(x + k, nx), x).wait_send()
            finish_copy(b, 0, x, x).wait_send()

    def drain(k, carry):
        for d, hop in ((2 * k + 1, 1), (2 * k + 2, 2)):
            for q in range(2):
                right_copy(d, hop, q, "wait_send")
            up_copy(tile_left(d), d - 1, x, "wait_send")
            down_copy(tile_left(d), d - 1, x, "wait_send")

            @pl.when(d < mid)
            def _():
                for q in range(2):
                    left_copy(d, hop, q, hop == 2, "wait_send")
                up_copy(tile_right(d), mid + d - 1, x, "wait_send")
                down_copy(tile_right(d), mid + d - 1, x, "wait_send")

        return carry

    with jax.named_scope("drain"):
        lax.fori_loop(0, levels, drain, 0)


def shards(nz, nx, hidden, lengths, attn_gain, w_query, w_latent, latent_gain, w_key, w_value, w_out):
    groups, rows, width = hidden.shape
    rank = w_latent.shape[2]
    cols = w_key.shape[2]
    heads = cols // HD
    share = rows // nx
    mine = groups * share
    half = width // 2
    mid = nz // 2
    vmem, dma = pltpu.VMEM, pltpu.SemaphoreType.DMA
    whole = pl.BlockSpec(memory_space=pltpu.VMEM)
    hbm = pl.BlockSpec(memory_space=pl.ANY)
    bf16, f32 = jnp.bfloat16, jnp.float32
    return pl.pallas_call(
        functools.partial(kernel, nz, nx),
        out_shape=(
            jax.ShapeDtypeStruct((groups, share, half), f32),
            jax.ShapeDtypeStruct((1, groups, rows, rank), f32),
        ),
        in_specs=[hbm] * 9,
        out_specs=(whole, whole),
        scratch_shapes=[
            pltpu.SMEM((groups,), jnp.int32),
            vmem((groups, rows, width), bf16),
            vmem((1, width), f32),
            vmem((1, rank), f32),
            vmem((width, cols), bf16),
            vmem((width, rank), bf16),
            vmem((rank, cols), bf16),
            vmem((rank, cols), bf16),
            vmem((cols, width), bf16),
            vmem((nx, mine, width), bf16),
            vmem((nz, nx, mine, rank), bf16),
            vmem((nx, mine, rank), bf16),
            vmem((groups, heads * rows, rank), bf16),
            vmem((groups, rank, heads * rows), bf16),
            vmem((3 * groups * rows, rank), bf16),
            vmem((rank, 3 * groups * rows), bf16),
            vmem((groups, 1, heads * rows), f32),
            vmem((groups, 1, heads * rows), f32),
            vmem((groups, rank, heads * rows), f32),
            vmem((rows, cols), bf16),
            vmem((groups, nx, 2, share, half), bf16),
            vmem((nx, groups, 2, share, half), bf16),
            vmem((2, mine, half), f32),
            vmem((mine, half), f32),
            vmem((nx, groups, share, half), bf16),
            dma((9,)),
            dma((mid, 2)),
            dma((mid, 2)),
            dma((mid, 2)),
            dma((mid, 2)),
            dma((nz - 1,)),
            dma((nz - 1,)),
            dma((nz - 1,)),
            dma((nz - 1,)),
            dma,
            dma,
            dma((groups, nx)),
            dma((groups, nx)),
            dma((nx,)),
            dma((nx,)),
            dma,
            dma,
            dma((groups, 2, nx)),
            dma((groups, nx)),
        ],
        compiler_params=pltpu.CompilerParams(
            collective_id=0, has_side_effects=True, vmem_limit_bytes=67043328
        ),
    )(lengths, hidden, attn_gain, w_query, w_latent, latent_gain, w_key, w_value, w_out)


def solution(mesh):
    return jax.shard_map(
        functools.partial(shards, mesh.shape["seq"], mesh.shape["head"]),
        mesh=mesh,
        in_specs=(
            P("rep", "seq", None),
            P("rep"),
            P("section", None),
            P("section", None, "head"),
            P("section", None, None),
            P("section", None),
            P("section", None, "head"),
            P("section", None, "head"),
            P("section", "head", None),
        ),
        out_specs=(P("rep", ("seq", "head"), "section"), P("section", "rep", "seq", None)),
        check_vma=False,
    )
```

time: 102 us -> 92.8 us (0.910)
  Pallas kernels: 97.6 us -> 88.7 us
    pallas_call x1, Pallas kernels: 97.6 us -> 88.7 us  [shards(): pl.pallas_call(functools.partial(kernel, nz, nx), out_shape=(jax.ShapeDty...]
where the time goes in v3:
time: 92.8 us; the launch traced here: 92.7 us
  Pallas kernels  88.7 us (96%)
  local copies, waits for them, and re-layouts  3.38 us (4%)
    pallas_call x1, Pallas kernels, shards(): pl.pallas_call(functools.partial(kernel, nz, nx), out_shape=(jax.ShapeDty...  88.7 us
    unnamed x2, local copies, waits for them, and re-layouts  3.38 us

profile of v3, /device:TPU:33, one launch (start us, length us, event | category | flops | bytes accessed | tf_op | source)
XLA Modules:
  0.0 92.7 jit_solution(9043754151052964179)
XLA Ops:
  0.6 88.7 %shard_map.104 = (f32[3,16,1024]{2,1,0:T(8,128)}, f32[1,3,64,512]{3,2,1,0:T(8,128)}) custom-call(s32[3]{0:T(128)} %len_hbm.1, bf16[3,64,2048]{2,1,0:T(8,128)(2,1)} %hid_hbm.1, f32[1,2048]{1,0:T(1,128)} %gain_hbm.1, bf16[1,2048,512]{2,1,0:T(8,128)(2,1)} %wq_hbm.1, bf16[1,2048,512]{2,1,0:T(8,128)(2,1)} %wl_hbm.1, f32[1,512]{1,0:T(1,128)} %lgain_hbm.1, ...), custom_call_target="tpu_custom_call" | custom-call | tf_op jit(solution)/shard_map/pallas_call | solution.py:500
  89.3 1.6 %copy.13 = f32[3,16,1024]{2,1,0:T(8,128)} copy(f32[3,16,1024]{2,1,0:T(8,128)} %get-tuple-element.4) | data formatting | bytes 393216
  90.9 1.8 %copy.14 = f32[1,3,64,512]{3,2,1,0:T(8,128)} copy(f32[1,3,64,512]{3,2,1,0:T(8,128)} %get-tuple-element.5) | data formatting | bytes 786432

commit v4 on v3

--- a/solution.py
+++ b/solution.py
@@ -28,8 +28,8 @@
 
 
 def kernel(
-    nz, nx, len_hbm, hid_hbm, gain_hbm, wq_hbm, wl_hbm, lgain_hbm, wk_hbm, wv_hbm, wo_hbm,
-    final, lat, lengths, hid, gain, lgain, wq, wl, wk, wv, wo, normed, kv, ownlat, absorbed, turned, last_keys, last_turned,
+    nz, nx, small, hid_hbm, wq_hbm, wl_hbm, wk_hbm, wv_hbm, wo_hbm,
+    final, lat, counts, hid, wq, wl, wk, wv, wo, normed, kv, ownlat, absorbed, turned, last_keys, last_turned,
     top, total, accum, attn, part, headsum, xkeep, xhalf, finsum, load_sem,
     r_send, r_recv, l_send, l_recv, xa_send, xa_recv, xb_send, xb_recv, seed_send, seed_recv,
     rs_send, rs_recv, ag_send, ag_recv, half_send, half_recv, fin_send, fin_recv,
@@ -51,7 +51,7 @@
         pltpu.make_async_copy(src, dst, load_sem.at[i])
         for i, (src, dst) in enumerate(
             [
-                (hid_hbm, hid), (gain_hbm, gain), (wl_hbm.at[0], wl), (lgain_hbm, lgain), (len_hbm, lengths),
+                (hid_hbm, hid), (small.at[:, width + rank:], counts), (wl_hbm.at[0], wl),
                 (wq_hbm.at[0], wq), (wk_hbm.at[0], wk), (wv_hbm.at[0], wv), (wo_hbm.at[0], wo),
             ]
         )
@@ -154,24 +154,25 @@
 
     def latents():
         flat = normed[...].reshape(nx * mine, width)
-        full = rms_scale(dot(flat, wl[...]), lgain[...])
+        full = rms_scale(dot(flat, wl[...]), lgain)
         for b, o, v in pieces(full):
             pos = z * rows + o * share + lax.broadcasted_iota(jnp.int32, (share, 1), 0)
             lat[0, b, o * share:(o + 1) * share] = jnp.where(pos < lengths[b], v, 0.0)
         return full.astype(jnp.bfloat16).reshape(nx, mine, rank)
 
+    gain, lgain = small[:, :width], small[:, width:width + rank]
     loads[0].wait()
     loads[1].wait()
+    lengths = [counts[0, b].astype(jnp.int32) for b in range(groups)]
 
     @pl.when(sec == 0)
     def _():
         for b in range(groups):
-            n = rms_scale(hid[b].astype(jnp.float32), gain[...]).astype(jnp.bfloat16)
+            n = rms_scale(hid[b].astype(jnp.float32), gain).astype(jnp.bfloat16)
             for o in range(nx):
                 normed[o, b * share:(b + 1) * share] = n[o * share:(o + 1) * share]
 
-    for load in loads[2:5]:
-        load.wait()
+    loads[2].wait()
 
     @pl.when(sec == 0)
     def _():
@@ -195,9 +196,9 @@
                     add = add + headsum[k, b, h].astype(jnp.float32)
                 halves.append(own[:, h * half:(h + 1) * half] + add)
                 xkeep[h, at] = halves[h]
-            n = rms_scale(jnp.concatenate(halves, axis=1), gain[...])
+            n = rms_scale(jnp.concatenate(halves, axis=1), gain)
             normed[x, at] = n.astype(jnp.bfloat16)
-        early = rms_scale(dot(normed[x], wl[...]), lgain[...])
+        early = rms_scale(dot(normed[x], wl[...]), lgain)
         kv[z, x] = early.astype(jnp.bfloat16)
         seed_copy(x).start()
 
@@ -255,13 +256,9 @@
         with jax.named_scope("agwait"):
             for k in range(1, nx):
                 normed_copy(x, lax.rem(x + k, nx)).wait_recv()
-        ownlat[...] = latents()
-        for k in range(2, nx):
-            o = lax.rem(x + k, nx)
-            kv[z, o] = ownlat[o]
-
-    loads[5].wait()
-    loads[6].wait()
+
+    loads[3].wait()
+    loads[4].wait()
     with jax.named_scope("query"):
         query = dot(normed[...].reshape(nx * mine, width), wq[...]).astype(jnp.bfloat16)
         for h in range(heads):
@@ -271,6 +268,16 @@
                 absorbed[b, h * rows + o * share:h * rows + (o + 1) * share] = v
         for b in range(groups):
             turned[b] = absorbed[b].T
+
+    arrive(1)
+
+    @pl.when(sec == 1)
+    def _():
+        with jax.named_scope("latents"):
+            ownlat[...] = latents()
+            for k in range(2, nx):
+                o = lax.rem(x + k, nx)
+                kv[z, o] = ownlat[o]
 
     key_at = lax.broadcasted_iota(jnp.int32, (rows, hrows), 0)
     row_at = lax.broadcasted_iota(jnp.int32, (rows, hrows), 1) % rows
@@ -334,7 +341,9 @@
         attend([z], True, False)
 
     def level(k, carry):
-        arrive(k)
+        @pl.when(k > 1)
+        def _():
+            arrive(k)
 
         def pair(d, c):
             with jax.named_scope("xwait"):
@@ -368,7 +377,7 @@
     last_turned[...] = end_turned
     all_later = z < mid - 1
 
-    for load in loads[7:]:
+    for load in loads[5:]:
         load.wait()
 
     def finish_copy(b, h, owner, source):
@@ -416,13 +425,39 @@
                     finish_copy(b, h, lax.rem(x + k, nx), x).start()
             finish_copy(b, 0, x, x).start()
 
+    def drain(k, carry):
+        for d, hop in ((2 * k + 1, 1), (2 * k + 2, 2)):
+            for q in range(2):
+                right_copy(d, hop, q, "wait_send")
+            up_copy(tile_left(d), d - 1, x, "wait_send")
+            down_copy(tile_left(d), d - 1, x, "wait_send")
+
+            @pl.when(d < mid)
+            def _():
+                for q in range(2):
+                    left_copy(d, hop, q, hop == 2, "wait_send")
+                up_copy(tile_right(d), mid + d - 1, x, "wait_send")
+                down_copy(tile_right(d), mid + d - 1, x, "wait_send")
+
+        return carry
+
+    with jax.named_scope("drain"):
+        lax.fori_loop(0, levels, drain, 0)
+
     @pl.when(sec == 0)
     def _():
         half_copy().wait_recv()
+        for b in range(groups):
+            for o in range(nx):
+                scatter_copy(b, o, x).wait_send()
 
     @pl.when(sec == 1)
     def _():
         xhalf[...] = xkeep[1]
+        half_copy().wait_send()
+        seed_copy(x).wait_send()
+        for k in range(1, nx):
+            normed_copy(lax.rem(x + k, nx), x).wait_send()
 
     for b in range(groups):
 
@@ -446,42 +481,13 @@
         pos = z * rows + x * share + lax.broadcasted_iota(jnp.int32, (share, 1), 0)
         final[b] = jnp.where(pos < lengths[b], xhalf[at] + add, 0.0)
 
-    @pl.when(sec == 0)
-    def _():
-        for b in range(groups):
-            for o in range(nx):
-                scatter_copy(b, o, x).wait_send()
-
     @pl.when(sec == 1)
     def _():
-        half_copy().wait_send()
-        seed_copy(x).wait_send()
-        for k in range(1, nx):
-            normed_copy(lax.rem(x + k, nx), x).wait_send()
         for b in range(groups):
             for k in range(1, nx):
                 for h in range(2):
                     finish_copy(b, h, lax.rem(x + k, nx), x).wait_send()
             finish_copy(b, 0, x, x).wait_send()
-
-    def drain(k, carry):
-        for d, hop in ((2 * k + 1, 1), (2 * k + 2, 2)):
-            for q in range(2):
-                right_copy(d, hop, q, "wait_send")
-            up_copy(tile_left(d), d - 1, x, "wait_send")
-            down_copy(tile_left(d), d - 1, x, "wait_send")
-
-            @pl.when(d < mid)
-            def _():
-                for q in range(2):
-                    left_copy(d, hop, q, hop == 2, "wait_send")
-                up_copy(tile_right(d), mid + d - 1, x, "wait_send")
-                down_copy(tile_right(d), mid + d - 1, x, "wait_send")
-
-        return carry
-
-    with jax.named_scope("drain"):
-        lax.fori_loop(0, levels, drain, 0)
 
 
 def shards(nz, nx, hidden, lengths, attn_gain, w_query, w_latent, latent_gain, w_key, w_value, w_out):
@@ -496,6 +502,8 @@
     vmem, dma = pltpu.VMEM, pltpu.SemaphoreType.DMA
     whole = pl.BlockSpec(memory_space=pltpu.VMEM)
     hbm = pl.BlockSpec(memory_space=pl.ANY)
+    counts = jnp.pad(lengths[None], ((0, 0), (0, 128 - groups))).astype(jnp.float32)
+    small = jnp.concatenate([attn_gain, latent_gain, counts], axis=1)
     bf16, f32 = jnp.bfloat16, jnp.float32
     return pl.pallas_call(
         functools.partial(kernel, nz, nx),
@@ -503,13 +511,11 @@
             jax.ShapeDtypeStruct((groups, share, half), f32),
             jax.ShapeDtypeStruct((1, groups, rows, rank), f32),
         ),
-        in_specs=[hbm] * 9,
+        in_specs=[whole] + [hbm] * 6,
         out_specs=(whole, whole),
         scratch_shapes=[
-            pltpu.SMEM((groups,), jnp.int32),
+            pltpu.SMEM((1, 128), f32),
             vmem((groups, rows, width), bf16),
-            vmem((1, width), f32),
-            vmem((1, rank), f32),
             vmem((width, cols), bf16),
             vmem((width, rank), bf16),
             vmem((rank, cols), bf16),
@@ -531,7 +537,7 @@
             vmem((2, mine, half), f32),
             vmem((mine, half), f32),
             vmem((nx, groups, share, half), bf16),
-            dma((9,)),
+            dma((7,)),
             dma((mid, 2)),
             dma((mid, 2)),
             dma((mid, 2)),
@@ -552,9 +558,9 @@
             dma((groups, nx)),
         ],
         compiler_params=pltpu.CompilerParams(
-            collective_id=0, has_side_effects=True, vmem_limit_bytes=67043328
+            collective_id=0, has_side_effects=True, vmem_limit_bytes=54500 * 1024
         ),
-    )(lengths, hidden, attn_gain, w_query, w_latent, latent_gain, w_key, w_value, w_out)
+    )(small, hidden, w_query, w_latent, w_key, w_value, w_out)
 
 
 def solution(mesh):

time: 92.8 us -> 92.6 us (level)
  local copies, waits for them, and re-layouts: 3.38 us -> 1.42 us
  other arithmetic: 0 us -> 1.38 us
    unnamed x2, local copies, waits for them, and re-layouts: 3.38 us -> 1.42 us
where the time goes in v4:
time: 92.6 us; the launch traced here: 92.5 us
  Pallas kernels  89 us (96%)
  local copies, waits for them, and re-layouts  1.42 us (2%)
  other arithmetic  1.38 us (1%)
    pallas_call x1, Pallas kernels, shards(): pl.pallas_call(functools.partial(kernel, nz, nx), out_shape=(jax.ShapeDty...  89 us

profile of v4, /device:TPU:33, one launch (start us, length us, event | category | flops | bytes accessed | tf_op | source)
XLA Modules:
  0.0 92.5 jit_solution(458421769258706765)
XLA Ops:
  0.6 0.7 pad_convert_fusion
  1.3 0.7 pad_maximum_fusion.small
  2.0 89.0 %shard_map.104 = (f32[3,16,1024]{2,1,0:T(8,128)S(1)}, f32[1,3,64,512]{3,2,1,0:T(8,128)S(1)}) custom-call(f32[1,2688]{1,0:T(1,128)S(1)} %pad_maximum_fusion.small, bf16[3,64,2048]{2,1,0:T(8,128)(2,1)} %hid_hbm.1, bf16[1,2048,512]{2,1,0:T(8,128)(2,1)} %wq_hbm.1, bf16[1,2048,512]{2,1,0:T(8,128)(2,1)} %wl_hbm.1, bf16[1,512,512]{2,1,0:T(8,128)(2,1)} %wk_hbm.1, ...), custom_call_target="tpu_custom_call" | custom-call | tf_op jit(solution)/shard_map/pallas_call | solution.py:508
  91.0 0.7 copy.13
  91.7 0.7 copy.14

commit v5 on v4

--- a/solution.py
+++ b/solution.py
@@ -29,7 +29,7 @@
 
 def kernel(
     nz, nx, small, hid_hbm, wq_hbm, wl_hbm, wk_hbm, wv_hbm, wo_hbm,
-    final, lat, counts, hid, wq, wl, wk, wv, wo, normed, kv, ownlat, absorbed, turned, last_keys, last_turned,
+    final_out, lat_out, final, lat, out_sem, counts, hid, wq, wl, wk, wv, wo, normed, kv, ownlat, absorbed, turned, last_keys, last_turned,
     top, total, accum, attn, part, headsum, xkeep, xhalf, finsum, load_sem,
     r_send, r_recv, l_send, l_recv, xa_send, xa_recv, xb_send, xb_recv, seed_send, seed_recv,
     rs_send, rs_recv, ag_send, ag_recv, half_send, half_recv, fin_send, fin_recv,
@@ -75,9 +75,9 @@
             src_ref=src, dst_ref=dst, send_sem=send, recv_sem=recv, device_id=to, device_id_type=MESH
         )
 
-    def scatter_copy(b, owner, source):
+    def scatter_copy(b, h, owner, source):
         return remote(
-            part.at[b, owner], headsum.at[source, b], rs_send.at[b, owner], rs_recv.at[b, source],
+            part.at[b, owner, h], headsum.at[source, b, h], rs_send.at[b, h, owner], rs_recv.at[b, h, source],
             {"section": other, "head": owner},
         )
 
@@ -151,6 +151,8 @@
         for o in range(nx):
             for b in range(groups):
                 yield b, o, values[(o * groups + b) * share:(o * groups + b + 1) * share]
+
+    lat_copy = pltpu.make_async_copy(lat, lat_out, out_sem.at[groups])
 
     def latents():
         flat = normed[...].reshape(nx * mine, width)
@@ -158,7 +160,20 @@
         for b, o, v in pieces(full):
             pos = z * rows + o * share + lax.broadcasted_iota(jnp.int32, (share, 1), 0)
             lat[0, b, o * share:(o + 1) * share] = jnp.where(pos < lengths[b], v, 0.0)
+        lat_copy.start()
         return full.astype(jnp.bfloat16).reshape(nx, mine, rank)
+
+    def normed_of(k):
+        o = lax.rem(x + k, nx)
+        at = pl.ds(pl.multiple_of(o * share, share), share)
+        raw = jnp.concatenate([hid[b, at].astype(jnp.float32) for b in range(groups)], axis=0)
+        normed[o] = rms_scale(raw, gain).astype(jnp.bfloat16)
+
+    def fill_own():
+        ownlat[...] = latents()
+        for k in range(2, nx):
+            o = lax.rem(x + k, nx)
+            kv[z, o] = ownlat[o]
 
     gain, lgain = small[:, :width], small[:, width:width + rank]
     loads[0].wait()
@@ -167,16 +182,17 @@
 
     @pl.when(sec == 0)
     def _():
-        for b in range(groups):
-            n = rms_scale(hid[b].astype(jnp.float32), gain).astype(jnp.bfloat16)
-            for o in range(nx):
-                normed[o, b * share:(b + 1) * share] = n[o * share:(o + 1) * share]
+        normed_of(0)
+        normed_of(1)
 
     loads[2].wait()
 
     @pl.when(sec == 0)
     def _():
-        kv[z] = latents()
+        rows_now = jnp.concatenate([normed[x], normed[x_up]], axis=0)
+        early = rms_scale(dot(rows_now, wl[...]), lgain).astype(jnp.bfloat16)
+        kv[z, x] = early[:mine]
+        kv[z, x_up] = early[mine:]
 
     with jax.named_scope("barrier"):
         pl.semaphore_wait(barrier, len(peers))
@@ -185,8 +201,9 @@
     def _():
         for b in range(groups):
             with jax.named_scope("rswait"):
-                for k in range(nx):
-                    scatter_copy(b, x, k).wait_recv()
+                for h in range(2):
+                    for k in range(nx):
+                        scatter_copy(b, h, x, k).wait_recv()
             at = pl.ds(b * share, share)
             own = hid[b, pl.ds(pl.multiple_of(x * share, share), share)].astype(jnp.float32)
             halves = []
@@ -249,6 +266,13 @@
                 left_copy(near, 0, q, False, "wait_recv")
                 across(tile_right(near), mid + near - 1, q)
 
+    @pl.when(sec == 0)
+    def _():
+        with jax.named_scope("fill"):
+            for k in range(2, nx):
+                normed_of(k)
+            fill_own()
+
     arrive(0)
 
     @pl.when(sec == 1)
@@ -256,6 +280,7 @@
         with jax.named_scope("agwait"):
             for k in range(1, nx):
                 normed_copy(x, lax.rem(x + k, nx)).wait_recv()
+        fill_own()
 
     loads[3].wait()
     loads[4].wait()
@@ -268,16 +293,6 @@
                 absorbed[b, h * rows + o * share:h * rows + (o + 1) * share] = v
         for b in range(groups):
             turned[b] = absorbed[b].T
-
-    arrive(1)
-
-    @pl.when(sec == 1)
-    def _():
-        with jax.named_scope("latents"):
-            ownlat[...] = latents()
-            for k in range(2, nx):
-                o = lax.rem(x + k, nx)
-                kv[z, o] = ownlat[o]
 
     key_at = lax.broadcasted_iota(jnp.int32, (rows, hrows), 0)
     row_at = lax.broadcasted_iota(jnp.int32, (rows, hrows), 1) % rows
@@ -341,9 +356,7 @@
         attend([z], True, False)
 
     def level(k, carry):
-        @pl.when(k > 1)
-        def _():
-            arrive(k)
+        arrive(k)
 
         def pair(d, c):
             with jax.named_scope("xwait"):
@@ -408,22 +421,21 @@
             for h in range(heads):
                 cols = slice(h * HD, (h + 1) * HD)
                 attn[:, cols] = dot(context[h * rows:(h + 1) * rows], wv[:, cols]).astype(jnp.bfloat16)
-            for h in range(2):
+        for h in range(2):
+            with jax.named_scope("out"):
                 out = dot(attn[...], wo[:, h * half:(h + 1) * half]).astype(jnp.bfloat16)
                 for o in range(nx):
                     part[b, o, h] = out[o * share:(o + 1) * share]
 
-        @pl.when(sec == 0)
-        def _():
-            for k in range(nx):
-                scatter_copy(b, lax.rem(x + nx - 1 - k, nx), x).start()
-
-        @pl.when(sec == 1)
-        def _():
-            for k in range(1, nx):
-                for h in range(2):
+            @pl.when(sec == 0)
+            def _():
+                for k in range(nx):
+                    scatter_copy(b, h, lax.rem(x + nx - 1 - k, nx), x).start()
+
+            @pl.when(sec == 1)
+            def _():
+                for k in range(1 if h == 1 else 0, nx):
                     finish_copy(b, h, lax.rem(x + k, nx), x).start()
-            finish_copy(b, 0, x, x).start()
 
     def drain(k, carry):
         for d, hop in ((2 * k + 1, 1), (2 * k + 2, 2)):
@@ -448,8 +460,9 @@
     def _():
         half_copy().wait_recv()
         for b in range(groups):
-            for o in range(nx):
-                scatter_copy(b, o, x).wait_send()
+            for h in range(2):
+                for o in range(nx):
+                    scatter_copy(b, h, o, x).wait_send()
 
     @pl.when(sec == 1)
     def _():
@@ -480,6 +493,7 @@
             add = add + finsum[k, b].astype(jnp.float32)
         pos = z * rows + x * share + lax.broadcasted_iota(jnp.int32, (share, 1), 0)
         final[b] = jnp.where(pos < lengths[b], xhalf[at] + add, 0.0)
+        pltpu.make_async_copy(final.at[b], final_out.at[b], out_sem.at[b]).start()
 
     @pl.when(sec == 1)
     def _():
@@ -488,6 +502,10 @@
                 for h in range(2):
                     finish_copy(b, h, lax.rem(x + k, nx), x).wait_send()
             finish_copy(b, 0, x, x).wait_send()
+
+    lat_copy.wait()
+    for b in range(groups):
+        pltpu.make_async_copy(final.at[b], final_out.at[b], out_sem.at[b]).wait()
 
 
 def shards(nz, nx, hidden, lengths, attn_gain, w_query, w_latent, latent_gain, w_key, w_value, w_out):
@@ -502,9 +520,15 @@
     vmem, dma = pltpu.VMEM, pltpu.SemaphoreType.DMA
     whole = pl.BlockSpec(memory_space=pltpu.VMEM)
     hbm = pl.BlockSpec(memory_space=pl.ANY)
-    counts = jnp.pad(lengths[None], ((0, 0), (0, 128 - groups))).astype(jnp.float32)
-    small = jnp.concatenate([attn_gain, latent_gain, counts], axis=1)
     bf16, f32 = jnp.bfloat16, jnp.float32
+    flat = ((0, 0, 0),)
+    pieces = (attn_gain, latent_gain, lengths[None])
+    size, at, small = width + rank + 128, 0, 0.0
+    for piece in pieces:
+        count = piece.shape[1]
+        zero = jnp.zeros((), piece.dtype)
+        small = small + lax.pad(piece, zero, flat + ((at, size - at - count, 0),)).astype(f32)
+        at += count
     return pl.pallas_call(
         functools.partial(kernel, nz, nx),
         out_shape=(
@@ -512,8 +536,11 @@
             jax.ShapeDtypeStruct((1, groups, rows, rank), f32),
         ),
         in_specs=[whole] + [hbm] * 6,
-        out_specs=(whole, whole),
+        out_specs=(hbm, hbm),
         scratch_shapes=[
+            vmem((groups, share, half), f32),
+            vmem((1, groups, rows, rank), f32),
+            dma((groups + 1,)),
             pltpu.SMEM((1, 128), f32),
             vmem((groups, rows, width), bf16),
             vmem((width, cols), bf16),
@@ -548,8 +575,8 @@
             dma((nz - 1,)),
             dma,
             dma,
-            dma((groups, nx)),
-            dma((groups, nx)),
+            dma((groups, 2, nx)),
+            dma((groups, 2, nx)),
             dma((nx,)),
             dma((nx,)),
             dma,

time: 92.6 us -> 91.1 us (0.984)
  no operation moved by 1% of the time
where the time goes in v5:
time: 91.1 us; the launch traced here: 91 us
  Pallas kernels  88.2 us (97%)
  local copies, waits for them, and re-layouts  1.42 us (2%)
    pallas_call x1, Pallas kernels, shards(): pl.pallas_call(functools.partial(kernel, nz, nx), out_shape=(jax.ShapeDty...  88.2 us

profile of v5, /device:TPU:33, one launch (start us, length us, event | category | flops | bytes accessed | tf_op | source)
XLA Modules:
  0.0 91.0 jit_solution(14179863683027573925)
XLA Ops:
  0.6 0.7 convert_add_fusion.small
  1.4 88.2 %shard_map.104 = (f32[3,16,1024]{2,1,0:T(8,128)S(1)}, f32[1,3,64,512]{3,2,1,0:T(8,128)S(1)}) custom-call(f32[1,2688]{1,0:T(1,128)S(1)} %convert_add_fusion.small, bf16[3,64,2048]{2,1,0:T(8,128)(2,1)} %hid_hbm.1, bf16[1,2048,512]{2,1,0:T(8,128)(2,1)} %wq_hbm.1, bf16[1,2048,512]{2,1,0:T(8,128)(2,1)} %wl_hbm.1, bf16[1,512,512]{2,1,0:T(8,128)(2,1)} %wk_hbm.1, ...), custom_call_target="tpu_custom_call" | custom-call | tf_op jit(solution)/shard_map/pallas_call | solution.py:532
  89.5 0.7 copy.13
  90.2 0.7 copy.14

commit v6 on v5

--- a/solution.py
+++ b/solution.py
@@ -29,10 +29,10 @@
 
 def kernel(
     nz, nx, small, hid_hbm, wq_hbm, wl_hbm, wk_hbm, wv_hbm, wo_hbm,
-    final_out, lat_out, final, lat, out_sem, counts, hid, wq, wl, wk, wv, wo, normed, kv, ownlat, absorbed, turned, last_keys, last_turned,
+    final, lat, counts, hid, wq, wl, wk, wv, wo, normed, kv, ownlat, absorbed, turned, last_keys, last_turned,
     top, total, accum, attn, part, headsum, xkeep, xhalf, finsum, load_sem,
     r_send, r_recv, l_send, l_recv, xa_send, xa_recv, xb_send, xb_recv, seed_send, seed_recv,
-    rs_send, rs_recv, ag_send, ag_recv, half_send, half_recv, fin_send, fin_recv,
+    sum_send, rs_recv, ag_send, ag_recv, half_send, half_recv, fin_recv,
 ):
     z, x, sec = lax.axis_index("seq"), lax.axis_index("head"), lax.axis_index("section")
     other = 1 - sec
@@ -46,6 +46,7 @@
     mid = nz // 2
     levels = mid // 2
     hrows = heads * rows
+    far_first = sorted(range(1, nx), key=lambda k: -min(k, nx - k))
 
     loads = [
         pltpu.make_async_copy(src, dst, load_sem.at[i])
@@ -56,7 +57,7 @@
             ]
         )
     ]
-    for load in loads:
+    for load in loads[:3]:
         load.start()
 
     main = mine - share
@@ -77,7 +78,7 @@
 
     def scatter_copy(b, h, owner, source):
         return remote(
-            part.at[b, owner, h], headsum.at[source, b, h], rs_send.at[b, h, owner], rs_recv.at[b, h, source],
+            part.at[b, owner, h], headsum.at[source, b, h], sum_send.at[b, h, owner], rs_recv.at[b, h, source],
             {"section": other, "head": owner},
         )
 
@@ -151,8 +152,6 @@
         for o in range(nx):
             for b in range(groups):
                 yield b, o, values[(o * groups + b) * share:(o * groups + b + 1) * share]
-
-    lat_copy = pltpu.make_async_copy(lat, lat_out, out_sem.at[groups])
 
     def latents():
         flat = normed[...].reshape(nx * mine, width)
@@ -160,7 +159,6 @@
         for b, o, v in pieces(full):
             pos = z * rows + o * share + lax.broadcasted_iota(jnp.int32, (share, 1), 0)
             lat[0, b, o * share:(o + 1) * share] = jnp.where(pos < lengths[b], v, 0.0)
-        lat_copy.start()
         return full.astype(jnp.bfloat16).reshape(nx, mine, rank)
 
     def normed_of(k):
@@ -186,6 +184,8 @@
         normed_of(1)
 
     loads[2].wait()
+    for load in loads[3:]:
+        load.start()
 
     @pl.when(sec == 0)
     def _():
@@ -219,22 +219,27 @@
         kv[z, x] = early.astype(jnp.bfloat16)
         seed_copy(x).start()
 
-    def first_sends(q):
+    def first_sends(hop, q):
+        right_copy(hop, hop, q, "start")
+        left_copy(hop, hop, q, hop == 2, "start")
+
+    @pl.when(sec == 0)
+    def _():
         for hop in (2, 1):
-            right_copy(hop, hop, q, "start")
-            left_copy(hop, hop, q, hop == 2, "start")
-
-    first_sends(0)
+            for q in range(2):
+                first_sends(hop, q)
 
     @pl.when(sec == 1)
     def _():
+        for hop in (2, 1):
+            first_sends(hop, 0)
         for k in range(1, nx):
             normed_copy(lax.rem(x + k, nx), x).start()
         half_copy().start()
         with jax.named_scope("seedwait"):
             seed_copy(x_up).wait_recv()
-
-    first_sends(1)
+        for hop in (2, 1):
+            first_sends(hop, 1)
 
     def arrive(k):
         near, deep = 2 * k + 1, 2 * k + 2
@@ -395,7 +400,7 @@
 
     def finish_copy(b, h, owner, source):
         return remote(
-            part.at[b, owner, h], finsum.at[source, b], fin_send.at[b, h, owner], fin_recv.at[b, source],
+            part.at[b, owner, h], finsum.at[source, b], sum_send.at[b, h, owner], fin_recv.at[b, source],
             {"section": h, "head": owner},
         )
 
@@ -429,12 +434,12 @@
 
             @pl.when(sec == 0)
             def _():
-                for k in range(nx):
-                    scatter_copy(b, h, lax.rem(x + nx - 1 - k, nx), x).start()
+                for k in far_first + [0]:
+                    scatter_copy(b, h, lax.rem(x + k, nx), x).start()
 
             @pl.when(sec == 1)
             def _():
-                for k in range(1 if h == 1 else 0, nx):
+                for k in far_first + [0] * (1 - h):
                     finish_copy(b, h, lax.rem(x + k, nx), x).start()
 
     def drain(k, carry):
@@ -493,7 +498,6 @@
             add = add + finsum[k, b].astype(jnp.float32)
         pos = z * rows + x * share + lax.broadcasted_iota(jnp.int32, (share, 1), 0)
         final[b] = jnp.where(pos < lengths[b], xhalf[at] + add, 0.0)
-        pltpu.make_async_copy(final.at[b], final_out.at[b], out_sem.at[b]).start()
 
     @pl.when(sec == 1)
     def _():
@@ -502,10 +506,6 @@
                 for h in range(2):
                     finish_copy(b, h, lax.rem(x + k, nx), x).wait_send()
             finish_copy(b, 0, x, x).wait_send()
-
-    lat_copy.wait()
-    for b in range(groups):
-        pltpu.make_async_copy(final.at[b], final_out.at[b], out_sem.at[b]).wait()
 
 
 def shards(nz, nx, hidden, lengths, attn_gain, w_query, w_latent, latent_gain, w_key, w_value, w_out):
@@ -536,11 +536,8 @@
             jax.ShapeDtypeStruct((1, groups, rows, rank), f32),
         ),
         in_specs=[whole] + [hbm] * 6,
-        out_specs=(hbm, hbm),
+        out_specs=(whole, whole),
         scratch_shapes=[
-            vmem((groups, share, half), f32),
-            vmem((1, groups, rows, rank), f32),
-            dma((groups + 1,)),
             pltpu.SMEM((1, 128), f32),
             vmem((groups, rows, width), bf16),
             vmem((width, cols), bf16),
@@ -581,7 +578,6 @@
             dma((nx,)),
             dma,
             dma,
-            dma((groups, 2, nx)),
             dma((groups, nx)),
         ],
         compiler_params=pltpu.CompilerParams(

time: 91.1 us -> 90.8 us (level)
  no operation moved by 1% of the time
where the time goes in v6:
time: 90.8 us; the launch traced here: 90.6 us
  Pallas kernels  87.8 us (97%)
  local copies, waits for them, and re-layouts  1.42 us (2%)
    pallas_call x1, Pallas kernels, shards(): pl.pallas_call(functools.partial(kernel, nz, nx), out_shape=(jax.ShapeDty...  87.8 us

profile of v6, /device:TPU:33, one launch (start us, length us, event | category | flops | bytes accessed | tf_op | source)
XLA Modules:
  0.0 90.6 jit_solution(7934111840859571302)
XLA Ops:
  0.6 0.7 convert_add_fusion.small
  1.4 87.8 %shard_map.104 = (f32[3,16,1024]{2,1,0:T(8,128)S(1)}, f32[1,3,64,512]{3,2,1,0:T(8,128)S(1)}) custom-call(f32[1,2688]{1,0:T(1,128)S(1)} %convert_add_fusion.small, bf16[3,64,2048]{2,1,0:T(8,128)(2,1)} %hid_hbm.1, bf16[1,2048,512]{2,1,0:T(8,128)(2,1)} %wq_hbm.1, bf16[1,2048,512]{2,1,0:T(8,128)(2,1)} %wl_hbm.1, bf16[1,512,512]{2,1,0:T(8,128)(2,1)} %wk_hbm.1, ...), custom_call_target="tpu_custom_call" | custom-call | tf_op jit(solution)/shard_map/pallas_call | solution.py:532
  89.2 0.7 copy.13
  89.9 0.7 copy.14

commit v7 on v6

--- a/solution.py
+++ b/solution.py
@@ -82,8 +82,9 @@
             {"section": other, "head": owner},
         )
 
-    def normed_copy(to, source):
-        return remote(normed.at[source], normed.at[source], ag_send.at[to], ag_recv.at[source], {"head": to})
+    def normed_copy(b, to, source):
+        spot = normed.at[source, pl.ds(b * share, share)]
+        return remote(spot, spot, ag_send.at[b, to], ag_recv.at[b, source], {"head": to})
 
     def half_copy():
         return remote(xkeep.at[0], xhalf, half_send, half_recv, {"section": other})
@@ -215,6 +216,9 @@
                 xkeep[h, at] = halves[h]
             n = rms_scale(jnp.concatenate(halves, axis=1), gain)
             normed[x, at] = n.astype(jnp.bfloat16)
+            if b + 1 < groups:
+                for k in far_first:
+                    normed_copy(b, lax.rem(x + k, nx), x).start()
         early = rms_scale(dot(normed[x], wl[...]), lgain)
         kv[z, x] = early.astype(jnp.bfloat16)
         seed_copy(x).start()
@@ -233,8 +237,8 @@
     def _():
         for hop in (2, 1):
             first_sends(hop, 0)
-        for k in range(1, nx):
-            normed_copy(lax.rem(x + k, nx), x).start()
+        for k in far_first:
+            normed_copy(groups - 1, lax.rem(x + k, nx), x).start()
         half_copy().start()
         with jax.named_scope("seedwait"):
             seed_copy(x_up).wait_recv()
@@ -278,14 +282,12 @@
                 normed_of(k)
             fill_own()
 
-    arrive(0)
-
     @pl.when(sec == 1)
     def _():
         with jax.named_scope("agwait"):
-            for k in range(1, nx):
-                normed_copy(x, lax.rem(x + k, nx)).wait_recv()
-        fill_own()
+            for b in range(groups):
+                for k in range(1, nx):
+                    normed_copy(b, x, lax.rem(x + k, nx)).wait_recv()
 
     loads[3].wait()
     loads[4].wait()
@@ -298,6 +300,13 @@
                 absorbed[b, h * rows + o * share:h * rows + (o + 1) * share] = v
         for b in range(groups):
             turned[b] = absorbed[b].T
+
+    arrive(0)
+
+    @pl.when(sec == 1)
+    def _():
+        with jax.named_scope("fill"):
+            fill_own()
 
     key_at = lax.broadcasted_iota(jnp.int32, (rows, hrows), 0)
     row_at = lax.broadcasted_iota(jnp.int32, (rows, hrows), 1) % rows
@@ -474,8 +483,9 @@
         xhalf[...] = xkeep[1]
         half_copy().wait_send()
         seed_copy(x).wait_send()
-        for k in range(1, nx):
-            normed_copy(lax.rem(x + k, nx), x).wait_send()
+        for b in range(groups):
+            for k in range(1, nx):
+                normed_copy(b, lax.rem(x + k, nx), x).wait_send()
 
     for b in range(groups):
 
@@ -574,8 +584,8 @@
             dma,
             dma((groups, 2, nx)),
             dma((groups, 2, nx)),
-            dma((nx,)),
-            dma((nx,)),
+            dma((groups, nx)),
+            dma((groups, nx)),
             dma,
             dma,
             dma((groups, nx)),

time: 90.8 us -> 91.9 us (1.012)
  Pallas kernels: 87.8 us -> 88.9 us
    pallas_call x1, Pallas kernels: 87.8 us -> 88.9 us  [shards(): pl.pallas_call(functools.partial(kernel, nz, nx), out_shape=(jax.ShapeDty...]
where the time goes in v7:
time: 91.9 us; the launch traced here: 91.7 us
  Pallas kernels  88.9 us (97%)
  local copies, waits for them, and re-layouts  1.42 us (2%)
    pallas_call x1, Pallas kernels, shards(): pl.pallas_call(functools.partial(kernel, nz, nx), out_shape=(jax.ShapeDty...  88.9 us

profile of v7, /device:TPU:33, one launch (start us, length us, event | category | flops | bytes accessed | tf_op | source)
XLA Modules:
  0.0 91.7 jit_solution(8223391055117752782)
XLA Ops:
  0.6 0.7 convert_add_fusion.small
  1.4 88.9 %shard_map.104 = (f32[3,16,1024]{2,1,0:T(8,128)S(1)}, f32[1,3,64,512]{3,2,1,0:T(8,128)S(1)}) custom-call(f32[1,2688]{1,0:T(1,128)S(1)} %convert_add_fusion.small, bf16[3,64,2048]{2,1,0:T(8,128)(2,1)} %hid_hbm.1, bf16[1,2048,512]{2,1,0:T(8,128)(2,1)} %wq_hbm.1, bf16[1,2048,512]{2,1,0:T(8,128)(2,1)} %wl_hbm.1, bf16[1,512,512]{2,1,0:T(8,128)(2,1)} %wk_hbm.1, ...), custom_call_target="tpu_custom_call" | custom-call | tf_op jit(solution)/shard_map/pallas_call | solution.py:542
  90.3 0.7 copy.13
  91.0 0.7 copy.14

commit v8 on v6

--- a/solution.py
+++ b/solution.py
@@ -48,16 +48,15 @@
     hrows = heads * rows
     far_first = sorted(range(1, nx), key=lambda k: -min(k, nx - k))
 
-    loads = [
-        pltpu.make_async_copy(src, dst, load_sem.at[i])
-        for i, (src, dst) in enumerate(
-            [
-                (hid_hbm, hid), (small.at[:, width + rank:], counts), (wl_hbm.at[0], wl),
-                (wq_hbm.at[0], wq), (wk_hbm.at[0], wk), (wv_hbm.at[0], wv), (wo_hbm.at[0], wo),
-            ]
-        )
-    ]
-    for load in loads[:3]:
+    cut = width // 4
+    moves = [(hid_hbm.at[b], hid.at[b]) for b in range(groups)]
+    moves += [(small.at[:, width + rank:], counts)]
+    moves += [(wl_hbm.at[0, pl.ds(i * cut, cut)], wl.at[pl.ds(i * cut, cut)]) for i in range(4)]
+    moves += [(wq_hbm.at[0], wq), (wk_hbm.at[0], wk), (wv_hbm.at[0], wv), (wo_hbm.at[0], wo)]
+    loads = [pltpu.make_async_copy(src, dst, load_sem.at[i]) for i, (src, dst) in enumerate(moves)]
+    latent_at = groups + 1
+    rest_at = latent_at + 4
+    for load in loads[:rest_at]:
         load.start()
 
     main = mine - share
@@ -174,8 +173,8 @@
             kv[z, o] = ownlat[o]
 
     gain, lgain = small[:, :width], small[:, width:width + rank]
-    loads[0].wait()
-    loads[1].wait()
+    for load in loads[:latent_at]:
+        load.wait()
     lengths = [counts[0, b].astype(jnp.int32) for b in range(groups)]
 
     @pl.when(sec == 0)
@@ -183,8 +182,9 @@
         normed_of(0)
         normed_of(1)
 
-    loads[2].wait()
-    for load in loads[3:]:
+    for load in loads[latent_at:rest_at]:
+        load.wait()
+    for load in loads[rest_at:]:
         load.start()
 
     @pl.when(sec == 0)
@@ -287,8 +287,8 @@
                 normed_copy(x, lax.rem(x + k, nx)).wait_recv()
         fill_own()
 
-    loads[3].wait()
-    loads[4].wait()
+    for load in loads[rest_at:rest_at + 2]:
+        load.wait()
     with jax.named_scope("query"):
         query = dot(normed[...].reshape(nx * mine, width), wq[...]).astype(jnp.bfloat16)
         for h in range(heads):
@@ -395,7 +395,7 @@
     last_turned[...] = end_turned
     all_later = z < mid - 1
 
-    for load in loads[5:]:
+    for load in loads[rest_at + 2:]:
         load.wait()
 
     def finish_copy(b, h, owner, source):
@@ -561,7 +561,7 @@
             vmem((2, mine, half), f32),
             vmem((mine, half), f32),
             vmem((nx, groups, share, half), bf16),
-            dma((7,)),
+            dma((groups + 9,)),
             dma((mid, 2)),
             dma((mid, 2)),
             dma((mid, 2)),

time: 90.8 us -> 90.9 us (level)
  no operation moved by 1% of the time
where the time goes in v8:
time: 90.9 us; the launch traced here: 90.7 us
  Pallas kernels  87.9 us (97%)
  local copies, waits for them, and re-layouts  1.42 us (2%)
    pallas_call x1, Pallas kernels, shards(): pl.pallas_call(functools.partial(kernel, nz, nx), out_shape=(jax.ShapeDty...  87.9 us

profile of v8, /device:TPU:33, one launch (start us, length us, event | category | flops | bytes accessed | tf_op | source)
XLA Modules:
  0.0 90.7 jit_solution(11571599146417542655)
XLA Ops:
  0.6 0.7 convert_add_fusion.small
  1.4 87.9 %shard_map.104 = (f32[3,16,1024]{2,1,0:T(8,128)S(1)}, f32[1,3,64,512]{3,2,1,0:T(8,128)S(1)}) custom-call(f32[1,2688]{1,0:T(1,128)S(1)} %convert_add_fusion.small, bf16[3,64,2048]{2,1,0:T(8,128)(2,1)} %hid_hbm.1, bf16[1,2048,512]{2,1,0:T(8,128)(2,1)} %wq_hbm.1, bf16[1,2048,512]{2,1,0:T(8,128)(2,1)} %wl_hbm.1, bf16[1,512,512]{2,1,0:T(8,128)(2,1)} %wk_hbm.1, ...), custom_call_target="tpu_custom_call" | custom-call | tf_op jit(solution)/shard_map/pallas_call | solution.py:532
  89.3 0.7 copy.13
  90.0 0.7 copy.14
